TPU v7x, 8 devices: a whole 2x2x1 slice. The times are simulated.
8 devices in a mesh: batch: 1 (over z), row: 2 (over y), col: 4 (over x, core).
Axes of the slice: x: 2, y: 2, z: 1, core: 2. Of those that a mesh axis runs over, the one named last changes fastest.
Arguments:
- lower_tri: bfloat16 [3072, 3072], P(('batch', 'row'), 'col')
- right_side: bfloat16 [3072, 16384], P(('batch', 'row'), 'col')
- grad_out: bfloat16 [3072, 16384], P(('batch', 'row'), 'col')
Outputs:
- output 1: bfloat16 [3072, 16384], P(('batch', 'row'), 'col')
- output 2: bfloat16 [3072, 3072], P(('batch', 'row'), 'col')
All inputs are finite; a program needn't handle non-finite values.
Results may differ from a plain program's by a relative error of at most 0.001.
Values are sent between devices in bfloat16 or wider.
A program may use at most 1 GiB of HBM per device.

v0:
```python
import jax
import jax.numpy as jnp
from jax import lax
from jax.sharding import PartitionSpec as P

BLOCK_SIZE = 256


def solution(mesh):
    mesh_rows = mesh.shape["row"]
    mesh_cols = mesh.shape["col"]
    group_size = max(mesh_rows, mesh_cols)
    row_step = group_size // mesh_rows
    col_step = group_size // mesh_cols
    block_spec = P(("batch", "row"), "col")

    def per_device(lower_tri, right_side, grad_out):
        rows_here, cols_here = lower_tri.shape
        num_cols = right_side.shape[1]
        num_steps = rows_here // (row_step * BLOCK_SIZE)
        right_pieces = []
        lower_pieces = []
        for step_idx in range(num_steps):
            first_row = step_idx * row_step * BLOCK_SIZE
            left_rows = rows_here - first_row
            grad_rows = grad_out[first_row:]
            lower_panel = lower_tri[first_row:, step_idx * col_step * BLOCK_SIZE:(step_idx + 1) * col_step * BLOCK_SIZE]
            gathered = lax.all_gather(lower_panel.reshape(left_rows, col_step, BLOCK_SIZE), "col", axis=2)
            right_part = jnp.einsum("rbqe,rf->bqef", gathered, grad_rows, preferred_element_type=jnp.float32)
            right_mine = lax.psum_scatter(right_part.reshape(row_step, mesh_rows * BLOCK_SIZE, num_cols), "row", scatter_dimension=1, tiled=True)
            right_pieces.append(right_mine.reshape(row_step * BLOCK_SIZE, num_cols).astype(jnp.bfloat16))
            side_block = right_side[first_row:first_row + row_step * BLOCK_SIZE].reshape(row_step, BLOCK_SIZE, num_cols)
            side_rows = lax.all_gather(side_block, "row", axis=1).reshape(col_step, mesh_cols, BLOCK_SIZE, num_cols)
            lower_part = jnp.einsum("rf,bqef->rbqe", grad_rows, side_rows, preferred_element_type=jnp.float32)
            lower_mine = lax.psum_scatter(lower_part.reshape(left_rows, col_step, mesh_cols * BLOCK_SIZE), "col", scatter_dimension=2, tiled=True)
            lower_piece = lower_mine.reshape(left_rows, col_step * BLOCK_SIZE).astype(jnp.bfloat16)
            lower_pieces.append(jnp.pad(lower_piece, ((first_row, 0), (0, 0))))
        grad_right = jnp.concatenate(right_pieces, axis=0)
        grad_lower = jnp.concatenate(lower_pieces, axis=1)
        row_pos = jnp.arange(rows_here)[:, None]
        col_pos = jnp.arange(cols_here)[None, :]
        row_global = (row_pos // BLOCK_SIZE * mesh_rows + lax.axis_index("row")) * BLOCK_SIZE + row_pos % BLOCK_SIZE
        col_global = (col_pos // BLOCK_SIZE * mesh_cols + lax.axis_index("col")) * BLOCK_SIZE + col_pos % BLOCK_SIZE
        grad_lower = jnp.where(row_global >= col_global, grad_lower, 0.0).astype(jnp.bfloat16)
        return grad_right, grad_lower

    return jax.shard_map(per_device, mesh=mesh, in_specs=(block_spec, block_spec, block_spec), out_specs=(block_spec, block_spec), check_vma=False)
```

profile of v0, /device:TPU:0, one launch (start us, length us, event | category | flops | bytes accessed | tf_op | source)
XLA Modules:
  0.0 1113.1 jit_solution(3198296602116544923)
XLA Ops:
  7.2 9.0 fusion.45
  20.6 100.9 %all-gather.14.cloned.1.call-done = bf16[2,2,256,4096]{3,2,1,0:T(8,128)(2,1)} async-done(((bf16[2,1,256,4096]{3,2,1,0:T(8,128)(2,1)}), bf16[2,2,256,4096]{3,2,1,0:T(8,128)(2,1)}) %all-gather.14.cloned.1.call-update) | async-done | bytes 8388624 | tf_op jit(solution)/shard_map/all_gather | solution.py:33
  121.5 10.5 fusion.20
  132.1 93.2 %all-gather.12.cloned.1.call-done = bf16[2,2,256,4096]{3,2,1,0:T(8,128)(2,1)} async-done(((bf16[2,1,256,4096]{3,2,1,0:T(8,128)(2,1)}), bf16[2,2,256,4096]{3,2,1,0:T(8,128)(2,1)}) %all-gather.12.cloned.1.call-update) | async-done | bytes 8388624 | tf_op jit(solution)/shard_map/all_gather | solution.py:33
  225.3 15.1 %fusion.17 = f32[1024,1,1024]{2,0,1:T(8,128)} fusion(bf16[1024,4096]{1,0:T(8,128)(2,1)} %bitcast.62, bf16[1536,4096]{1,0:T(8,128)(2,1)} %param.5), kind=kOutput, calls=%fused_computation.23 | convolution fusion | flops 8589934592 | bytes 20971520 | tf_op jit(solution)/shard_map/rf,bqef->rbqe/dot_general | solution.py:34
  240.7 89.0 %all-gather.10.cloned.1.call-done = bf16[2,2,256,4096]{3,2,1,0:T(8,128)(2,1)} async-done(((bf16[2,1,256,4096]{3,2,1,0:T(8,128)(2,1)}), bf16[2,2,256,4096]{3,2,1,0:T(8,128)(2,1)}) %all-gather.10.cloned.1.call-update) | async-done | bytes 8388624 | tf_op jit(solution)/shard_map/all_gather | solution.py:33
  329.7 19.6 %convolution_bitcast_fusion = f32[1536,1,1024]{2,0,1:T(8,128)} fusion(bf16[1536,4096]{1,0:T(8,128)(2,1)} %param.5, bf16[1024,4096]{1,0:T(8,128)(2,1)} %bitcast.61), kind=kOutput, calls=%fused_computation.15 | convolution fusion | flops 12884901888 | bytes 27262976 | tf_op jit(solution)/shard_map/rf,bqef->rbqe/dot_general | solution.py:34
  350.9 10.2 fusion.10
  361.2 5.0 all-gather.18.cloned.1.call-done
  369.0 14.5 %fusion.2 = f32[2,512,4096]{2,1,0:T(8,128)} fusion(bf16[2,512,1024]{2,1,0:T(8,128)(2,1)S(1)} %bitcast.59, bf16[1536,4096]{1,0:T(8,128)(2,1)} %param.5), kind=kOutput, calls=%fused_computation.3 | convolution fusion | flops 8589934592 | bytes 27262976 | tf_op jit(solution)/shard_map/rbqe,rf->bqef/dot_general | solution.py:29
  383.8 9.6 all-gather.16.cloned.1.call-done
  393.4 3.2 copy.11
  396.6 19.4 %fusion = f32[2,512,4096]{2,1,0:T(8,128)} fusion(bf16[2,512,1536]{2,1,0:T(8,128)(2,1)S(1)} %bitcast.58, bf16[1536,4096]{1,0:T(8,128)(2,1)} %param.5), kind=kOutput, calls=%fused_computation.1 | convolution fusion | flops 12884901888 | bytes 32505856 | tf_op jit(solution)/shard_map/rbqe,rf->bqef/dot_general | solution.py:29
  416.0 6.0 reduce-scatter.17.cloned.1.call-done
  423.1 39.7 %reduce-scatter.15.cloned.1.call-done = f32[1024,1,256]{2,0,1:T(8,128)} async-done(((f32[1024,1,1024]{2,0,1:T(8,128)}), f32[1024,1,256]{2,0,1:T(8,128)}) %reduce-scatter.15.cloned.1.call-update) | async-done | bytes 1048592 | tf_op jit(solution)/shard_map/reduce_scatter | solution.py:35
  464.1 53.1 %reduce-scatter.13.cloned.1.call-done = f32[1536,1,256]{2,0,1:T(8,128)} async-done(((f32[1536,1,1024]{2,0,1:T(8,128)}), f32[1536,1,256]{2,0,1:T(8,128)}) %reduce-scatter.13.cloned.1.call-update) | async-done | bytes 1572880 | tf_op jit(solution)/shard_map/reduce_scatter | solution.py:35
  518.7 2.9 compare_select_fusion
  521.6 184.1 %reduce-scatter.11.cloned.1.call-done = f32[2,256,4096]{2,1,0:T(8,128)} async-done(((f32[2,512,4096]{2,1,0:T(8,128)}), f32[2,256,4096]{2,1,0:T(8,128)}) %reduce-scatter.11.cloned.1.call-update) | async-done | bytes 8388624 | tf_op jit(solution)/shard_map/reduce_scatter | solution.py:30
  705.7 6.0 convert_element_type.46
  711.7 182.6 %reduce-scatter.9.cloned.1.call-done = f32[2,256,4096]{2,1,0:T(8,128)} async-done(((f32[2,512,4096]{2,1,0:T(8,128)}), f32[2,256,4096]{2,1,0:T(8,128)}) %reduce-scatter.9.cloned.1.call-update) | async-done | bytes 8388624 | tf_op jit(solution)/shard_map/reduce_scatter | solution.py:30
  894.3 6.1 convert_element_type.44
  900.3 182.4 %reduce-scatter.7.cloned.1.call-done = f32[2,256,4096]{2,1,0:T(8,128)} async-done(((f32[2,512,4096]{2,1,0:T(8,128)}), f32[2,256,4096]{2,1,0:T(8,128)}) %reduce-scatter.7.cloned.1.call-update) | async-done | bytes 8388624 | tf_op jit(solution)/shard_map/reduce_scatter | solution.py:30
  1082.8 4.1 convert_element_type.42
  1088.6 17.7 %pad_maximum_fusion = bf16[1536,4096]{1,0:T(8,128)(2,1)} fusion(bf16[512,4096]{1,0:T(8,128)(2,1)S(1)} %bitcast.52, bf16[512,4096]{1,0:T(8,128)(2,1)S(1)} %bitcast.53, bf16[512,4096]{1,0:T(8,128)(2,1)S(1)} %bitcast.54), kind=kLoop, calls=%fused_computation | loop fusion | flops 37748736 | bytes 25165824 | tf_op jit(solution)/shard_map/concatenate | solution.py:38
  (41 shorter events, 15.0 us)
Async XLA Ops:
  7.2 114.3 %all-gather.14.cloned.1.call-start = ((), (), s32[]{:S(2)}) async-start(), calls=%async_computation.13 | async-start | bytes 12582912 | tf_op jit(solution)/shard_map/all_gather | solution.py:33
  16.2 1.7 copy-start.2
  16.2 209.1 %all-gather.12.cloned.1.call-start = ((), (), s32[]{:S(2)}) async-start(), calls=%async_computation.11 | async-start | bytes 12582912 | tf_op jit(solution)/shard_map/all_gather | solution.py:33
  17.0 312.7 %all-gather.10.cloned.1.call-start = ((), (), s32[]{:S(2)}) async-start(), calls=%async_computation.9 | async-start | bytes 12582912 | tf_op jit(solution)/shard_map/all_gather | solution.py:33
  17.7 331.6 %all-gather.20.cloned.1.call-start = ((), (), s32[]{:S(2)}) async-start(), calls=%async_computation.17 | async-start | bytes 1310720 | tf_op jit(solution)/shard_map/all_gather | solution.py:28
  18.7 347.5 %all-gather.18.cloned.1.call-start = ((), (), s32[]{:S(2)}) async-start(), calls=%async_computation.16 | async-start | bytes 2621440 | tf_op jit(solution)/shard_map/all_gather | solution.py:28
  19.6 373.9 %all-gather.16.cloned.1.call-start = ((), (), s32[]{:S(2)}) async-start(), calls=%async_computation.15 | async-start | bytes 3932160 | tf_op jit(solution)/shard_map/all_gather | solution.py:28
  20.6 401.4 %reduce-scatter.17.cloned.1.call-start = ((), (), s32[]{:S(2)}) async-start(), calls=%async_computation.14 | async-start | bytes 2621440 | tf_op jit(solution)/shard_map/reduce_scatter | solution.py:35
  132.0 330.8 %reduce-scatter.15.cloned.1.call-start = ((), (), s32[]{:S(2)}) async-start(), calls=%async_computation.12 | async-start | bytes 5242880 | tf_op jit(solution)/shard_map/reduce_scatter | solution.py:35
  240.4 276.8 %reduce-scatter.13.cloned.1.call-start = ((), (), s32[]{:S(2)}) async-start(), calls=%async_computation.10 | async-start | bytes 7864320 | tf_op jit(solution)/shard_map/reduce_scatter | solution.py:35
  349.3 356.4 %reduce-scatter.11.cloned.1.call-start = ((), (), s32[]{:S(2)}) async-start(), calls=%async_computation.8 | async-start | bytes 25165824 | tf_op jit(solution)/shard_map/reduce_scatter | solution.py:30
  361.1 533.1 %reduce-scatter.9.cloned.1.call-start = ((), (), s32[]{:S(2)}) async-start(), calls=%async_computation.7 | async-start | bytes 25165824 | tf_op jit(solution)/shard_map/reduce_scatter | solution.py:30
  383.5 699.3 %reduce-scatter.7.cloned.1.call-start = ((), (), s32[]{:S(2)}) async-start(), calls=%async_computation.6 | async-start | bytes 25165824 | tf_op jit(solution)/shard_map/reduce_scatter | solution.py:30
  1082.8 4.6 copy-start
  1082.8 5.9 copy-start.1
Sparse Core Ops, SparseCore 0:
  16.4 105.0 all-gather.13
  123.0 102.2 all-gather.11
  227.4 102.2 all-gather.9
  331.1 13.8 all-gather.19
  346.3 19.7 all-gather.17
  367.5 25.8 all-gather.15
  396.5 25.4 reduce-scatter.16
  424.5 38.2 reduce-scatter.14
  465.9 51.2 reduce-scatter.12
  519.3 186.2 reduce-scatter.10
  707.9 186.2 reduce-scatter.8
  896.4 186.3 reduce-scatter.6
where the time goes:
time: 1110 us
  waiting for transfers between devices  947 us (85%)
  matrix products  89.2 us (8%)
  other arithmetic  40.7 us (4%)
  local copies, waits for them, and re-layouts  20.8 us (2%)
  between operations  14.3 us (1%)
    reduce_scatter x3, waiting for transfers between devices, per_device(): lax.psum_scatter(right_part.reshape(row_step, mesh_rows * BLOCK_SIZE, num...  549 us
    all_gather x3, waiting for transfers between devices, per_device(): lax.all_gather(side_block, 'row', axis=1)  283 us
    reduce_scatter x3, waiting for transfers between devices, per_device(): lax.psum_scatter(lower_part.reshape(left_rows, col_step, mesh_cols * BLOC...  98.8 us
    dot_general x3, matrix products, per_device(): jnp.einsum('rf,bqef->rbqe', grad_rows, side_rows, preferred_element_type=...  45.2 us
    dot_general x3, matrix products, per_device(): jnp.einsum('rbqe,rf->bqef', gathered, grad_rows, preferred_element_type=j...  44.1 us
  transfers between devices with their start and end apart: 12, of which 11 were waited for; matrix products, arithmetic and copies ran while one was open for 11% of the time, Pallas kernels for 0%

commit v1 on v0

v1 whole, which is shorter than its diff:
```python
import jax
import jax.numpy as jnp
from jax import lax
from jax.experimental import pallas as pl
from jax.experimental.pallas import tpu as pltpu
from jax.sharding import PartitionSpec as P

MESH = pl.DeviceIdType.MESH
BLOCK = 256
NUM = 6
COLS = 4096
TILE = 512
VMEM_BYTES = 67043328
PANEL_START = (0, 6, 10)
FINAL_START = (0, 1, 2, 4, 6, 9)
COMMON = {(1, 0): 0, (2, 0): 1, (3, 0): 2, (3, 1): 3, (4, 0): 4, (4, 1): 5, (5, 0): 6, (5, 1): 7, (5, 2): 8}


def packed_row(p, m):
    return (PANEL_START[p] + m - 2 * p) * BLOCK


def dot_nt(lhs, rhs):
    return lax.dot_general(lhs, rhs, (((1,), (1,)), ((), ())), preferred_element_type=jnp.float32)


def kernel(lower, right, grad, out_right, out_same, out_cross, out_diag,
           grad_v, right_v, other_v, lower_v, slot, hop, fin_same, fin_cross, fin_diag, total, stage, turned,
           grad_send, grad_recv, load_sem, low_load, low_cross_send, low_cross_recv, low_send, low_recv,
           core_send, core_recv, hop_send, hop_recv, out_sem, fin_sem, core_free, hop_free):
    row = lax.axis_index("row")
    col = lax.axis_index("col")
    x = col // 2
    owner = (col % 2) == row
    guest = jnp.logical_not(owner)
    to_row = {"row": 1 - row}
    to_core = {"col": col + 1 - 2 * (col % 2)}
    to_chip = {"col": lax.rem(col + 2, 4)}

    def remote(src, dst, send, recv, where):
        return pltpu.make_async_remote_copy(src_ref=src, dst_ref=dst, send_sem=send, recv_sem=recv, device_id=where, device_id_type=MESH)

    def send_grad(m):
        return remote(grad.at[pl.ds(m * BLOCK, BLOCK)], other_v.at[pl.ds(m * BLOCK, BLOCK)], grad_send.at[m], grad_recv.at[m], to_row)

    def panel_src(p):
        return lower.at[pl.ds(2 * p * BLOCK, (NUM - 2 * p) * BLOCK), pl.ds(p * BLOCK, BLOCK)]

    def panel_dst(parity, p):
        return lower_v.at[x, parity, pl.ds(PANEL_START[p] * BLOCK, (NUM - 2 * p) * BLOCK)]

    def send_panel(p):
        return remote(panel_src(p), panel_dst(1, p), low_cross_send.at[p], low_cross_recv.at[p], to_row)

    def send_low(index, half, where):
        return remote(lower_v.at[half], lower_v.at[half], low_send.at[index], low_recv.at[index], where)

    def load(src, dst, m, k):
        return pltpu.make_async_copy(src.at[pl.ds(m * BLOCK, BLOCK)], dst.at[pl.ds(m * BLOCK, BLOCK)], load_sem.at[k, m])

    def send_core(group, m):
        part = slot.at[pl.ds(m * (m + 1) // 2, m + 1)]
        return remote(part, part, core_send.at[group, m], core_recv.at[group, m], to_core)

    def send_hop(group, m, side):
        base = m * (m + 1) // 2
        first, count = (base + m // 2 + 1, (m + 1) // 2) if side == 0 else (base, m // 2 + 1)
        return remote(slot.at[pl.ds(first, count)], hop.at[pl.ds(FINAL_START[m], count)], hop_send.at[group, m], hop_recv.at[group, m], to_chip)

    barrier = pltpu.get_barrier_semaphore()
    for where in (to_row, to_core, to_chip):
        pl.semaphore_signal(barrier, inc=1, device_id=where, device_id_type=MESH)
    pl.semaphore_wait(barrier, 3)

    @pl.when(guest)
    def _():
        for p in range(3):
            send_panel(p).start()

    for m in range(NUM - 1, 0, -1):
        send_grad(m).start()

    @pl.when(row == 1)
    def _():
        send_grad(0).start()

    for m in range(NUM):
        load(grad, grad_v, m, 0).start()
        load(right, right_v, m, 1).start()

    @pl.when(owner)
    def _():
        for p in range(3):
            pltpu.make_async_copy(panel_src(p), panel_dst(0, p), low_load.at[p]).start()

    def partial_sums(source, group, m):
        @pl.when(owner)
        def _():
            send_core(group, m).wait_recv()

        def one(n, carry):
            index = m * (m + 1) // 2 + (n % 2) * (m // 2 + 1) + n // 2
            value = dot_nt(source[pl.ds(m * BLOCK, BLOCK), :], right_v[pl.ds(pl.multiple_of(n * BLOCK, BLOCK), BLOCK), :])
            slot[index] = jnp.where(owner, slot[index], 0.0) + value
            return carry

        lax.fori_loop(0, m + 1, one, 0)

        @pl.when(guest)
        def _():
            send_core(group, m).start()

        for side in range(2):
            if side == 1 or m > 0:
                @pl.when(jnp.logical_and(owner, x == side))
                def _(side=side):
                    send_hop(group, m, side).start()

    def finish(group, m):
        for side in range(2):
            @pl.when(jnp.logical_and(owner, x == side))
            def _(side=side):
                if side == 0 or m > 0:
                    send_hop(group, m, 1 - side).wait_recv()
                if side == 1 or m > 0:
                    send_hop(group, m, side).wait_send()
                for p in range(m // 2 + 1):
                    n = 2 * p + side
                    target, place = (fin_cross, COMMON[m, p]) if (m, p) in COMMON else (fin_diag, m // 2)
                    if group == 0:
                        target, place = fin_same, FINAL_START[m] + p
                    if n > m:
                        target[place] = jnp.zeros((BLOCK, BLOCK), jnp.bfloat16)
                        continue
                    value = slot[m * (m + 1) // 2 + side * (m // 2 + 1) + p] + hop[FINAL_START[m] + p]
                    if n == m and group == 0:
                        rows = lax.broadcasted_iota(jnp.int32, (BLOCK, BLOCK), 0)
                        cols = lax.broadcasted_iota(jnp.int32, (BLOCK, BLOCK), 1)
                        value = jnp.where(rows >= cols, value, 0.0)
                    if n == m and group == 1:
                        value = jnp.where(row == 0, value, 0.0)
                    target[place] = value.astype(jnp.bfloat16)

    for m in range(NUM):
        load(grad, grad_v, m, 0).wait()
        load(right, right_v, m, 1).wait()
        partial_sums(grad_v, 0, m)

    @pl.when(owner)
    def _():
        for p in range(3):
            pltpu.make_async_copy(panel_src(p), panel_dst(0, p), low_load.at[p]).wait()
            send_panel(p).wait_recv()
        send_low(0, x, to_chip).start()
        send_low(1, x, to_core).start()

    for m in range(NUM):
        finish(0, m)

    @pl.when(owner)
    def _():
        pl.semaphore_signal(core_free, inc=1, device_id=to_core, device_id_type=MESH)
        pl.semaphore_signal(hop_free, inc=1, device_id=to_chip, device_id_type=MESH)
        send_low(0, 1 - x, to_chip).wait_recv()
        send_low(2, 1 - x, to_core).start()
        pl.semaphore_wait(hop_free, 1)

    @pl.when(guest)
    def _():
        send_low(1, x, to_core).wait_recv()
        send_low(2, 1 - x, to_core).wait_recv()
        for m in range(NUM):
            send_core(0, m).wait_send()
        pl.semaphore_wait(core_free, 1)

    def turn(n):
        p, half = n // 2, n % 2
        for parity in range(2):
            for m in range(n, NUM):
                turned[parity, :, pl.ds((m - n) * BLOCK, BLOCK)] = lower_v[half, parity, pl.ds(packed_row(p, m), BLOCK), :].T

    def put(n):
        return pltpu.make_async_copy(stage, out_right.at[pl.ds(n * BLOCK, BLOCK)], out_sem)

    def tiles(body):
        def one(t, carry):
            body(pl.ds(pl.multiple_of(t * TILE, TILE), TILE))
            return carry
        lax.fori_loop(0, COLS // TILE, one, 0)

    for m in range(NUM - 1, 0, -1):
        send_grad(m).wait_recv()
        partial_sums(other_v, 1, m)
        turn(m)
        if m < NUM - 1:
            put(m + 1).wait()
        depth = (NUM - m) * BLOCK

        def product(cols, m=m, depth=depth):
            value = jnp.dot(turned[0, :, :depth], grad_v[m * BLOCK:, cols], preferred_element_type=jnp.float32)
            value += jnp.dot(turned[1, :, :depth], other_v[m * BLOCK:, cols], preferred_element_type=jnp.float32)
            stage[:, cols] = value.astype(jnp.bfloat16)

        tiles(product)
        put(m).start()
        if m < NUM - 1:
            finish(1, m + 1)

    turn(0)

    def all_but_last(cols):
        value = jnp.dot(turned[0], grad_v[:, cols], preferred_element_type=jnp.float32)
        total[:, cols] = value + jnp.dot(turned[1, :, BLOCK:], other_v[BLOCK:, cols], preferred_element_type=jnp.float32)

    tiles(all_but_last)
    finish(1, 1)
    put(1).wait()

    @pl.when(row == 0)
    def _():
        send_grad(0).wait_recv()
        partial_sums(other_v, 1, 0)

        def last(cols):
            value = jnp.dot(turned[1, :, :BLOCK], other_v[:BLOCK, cols], preferred_element_type=jnp.float32)
            stage[:, cols] = (total[:, cols] + value).astype(jnp.bfloat16)

        tiles(last)
        put(0).start()
        finish(1, 0)

    @pl.when(row == 1)
    def _():
        def last(cols):
            stage[:, cols] = total[:, cols].astype(jnp.bfloat16)

        tiles(last)
        put(0).start()
        fin_diag[0] = jnp.zeros((BLOCK, BLOCK), jnp.bfloat16)

    @pl.when(owner)
    def _():
        copies = [pltpu.make_async_copy(src, dst, fin_sem.at[k])
                  for k, (src, dst) in enumerate(((fin_same, out_same), (fin_cross, out_cross), (fin_diag, out_diag)))]
        for copy in copies:
            copy.start()
        for copy in copies:
            copy.wait()

    put(0).wait()
    for m in range(NUM - 1, 0, -1):
        send_grad(m).wait_send()

    @pl.when(row == 1)
    def _():
        send_grad(0).wait_send()

    @pl.when(owner)
    def _():
        send_low(0, x, to_chip).wait_send()
        send_low(1, x, to_core).wait_send()
        send_low(2, 1 - x, to_core).wait_send()

    @pl.when(guest)
    def _():
        for p in range(3):
            send_panel(p).wait_send()
        for m in range(1, NUM):
            send_core(1, m).wait_send()

        @pl.when(row == 0)
        def _():
            send_core(1, 0).wait_send()


def solution(mesh):
    block_spec = P(("batch", "row"), "col")
    device = lambda row, col: row * 4 + col
    owners = [(row, 2 * chip + row) for row in range(2) for chip in range(2)]
    return_pairs = [(device(row, col), device(1 - row, col)) for row, col in owners]
    return_pairs_down = [(src, dst) for src, dst in return_pairs if src < 4]

    def per_device(lower_tri, right_side, grad_out):
        bf16, f32 = jnp.bfloat16, jnp.float32
        dma = pltpu.SemaphoreType.DMA
        block = lambda count: jax.ShapeDtypeStruct((count, BLOCK, BLOCK), bf16)
        hbm = pl.BlockSpec(memory_space=pl.ANY)
        grad_right, same, cross, diag = pl.pallas_call(
            kernel,
            out_shape=(jax.ShapeDtypeStruct(grad_out.shape, bf16), block(12), block(9), block(3)),
            in_specs=[hbm] * 3,
            out_specs=[hbm] * 4,
            scratch_shapes=[
                pltpu.VMEM((NUM * BLOCK, COLS), bf16), pltpu.VMEM((NUM * BLOCK, COLS), bf16), pltpu.VMEM((NUM * BLOCK, COLS), bf16),
                pltpu.VMEM((2, 2, 12 * BLOCK, BLOCK), bf16),
                pltpu.VMEM((21, BLOCK, BLOCK), f32), pltpu.VMEM((12, BLOCK, BLOCK), f32),
                pltpu.VMEM((12, BLOCK, BLOCK), bf16), pltpu.VMEM((9, BLOCK, BLOCK), bf16), pltpu.VMEM((3, BLOCK, BLOCK), bf16),
                pltpu.VMEM((BLOCK, COLS), f32), pltpu.VMEM((BLOCK, COLS), bf16), pltpu.VMEM((2, BLOCK, NUM * BLOCK), bf16),
                dma((NUM,)), dma((NUM,)), dma((2, NUM)), dma((3,)), dma((3,)), dma((3,)), dma((3,)), dma((3,)),
                dma((2, NUM)), dma((2, NUM)), dma((2, NUM)), dma((2, NUM)), dma, dma((3,)),
                pltpu.SemaphoreType.REGULAR, pltpu.SemaphoreType.REGULAR,
            ],
            compiler_params=pltpu.CompilerParams(collective_id=1, has_side_effects=True, vmem_limit_bytes=VMEM_BYTES),
        )(lower_tri, right_side, grad_out)

        got = lax.ppermute(cross, ("row", "col"), return_pairs)
        got_diag = lax.ppermute(diag, ("row", "col"), return_pairs_down)
        row, col = lax.axis_index("row"), lax.axis_index("col")
        is_owner = (col % 2) == row
        zero = jnp.zeros((BLOCK, BLOCK), bf16)

        def piece(m, p):
            if p > m // 2:
                return zero
            moved = got[COMMON[m, p]] if (m, p) in COMMON else got_diag[m // 2]
            return jnp.where(is_owner, same[FINAL_START[m] + p], moved)

        grad_lower = jnp.concatenate([jnp.concatenate([piece(m, p) for p in range(3)], axis=1) for m in range(NUM)], axis=0)
        return grad_right, grad_lower

    return jax.shard_map(per_device, mesh=mesh, in_specs=(block_spec, block_spec, block_spec), out_specs=(block_spec, block_spec), check_vma=False)
```

time: 1110 us -> 342 us (0.31)
  waiting for transfers between devices: 947 us -> 16.5 us
  Pallas kernels: 0 us -> 308 us
  matrix products: 89.2 us -> 0 us
  other arithmetic: 40.7 us -> 1.37 us
  between operations: 14.3 us -> 0.77 us
    reduce_scatter x6 -> x0, waiting for transfers between devices: 648 us -> none  [the longest x3 549 us: per_device(): lax.psum_scatter(right_part.reshape(row_step, mesh_rows * BLOCK_SIZE, num...]
    pallas_call x0 -> x1, Pallas kernels: none -> 308 us  [per_device(): pl.pallas_call(kernel, out_shape=(jax.ShapeDtypeStruct(grad_out.shape, bf...]
    all_gather x6 -> x0, waiting for transfers between devices: 298 us -> none  [the longest x3 283 us: per_device(): lax.all_gather(side_block, 'row', axis=1)]
    dot_general x6 -> x0, matrix products: 89.2 us -> none  [the longest x3 45.2 us: per_device(): jnp.einsum('rf,bqef->rbqe', grad_rows, side_rows, preferred_element_type=...]
    convert_element_type x6 -> x0, other arithmetic: 20.1 us -> none  [the longest x3 16.2 us: per_device(): right_mine.reshape(row_step * BLOCK_SIZE, num_cols).astype(jnp.bfloat16)]
    concatenate x1, other arithmetic: 17.7 us -> 0.03 us  [per_device(): jnp.concatenate([jnp.concatenate([piece(m, p) for p in range(3)], axis=1)...]
    ppermute x0 -> x2, waiting for transfers between devices: none -> 16.5 us  [the longest x1 16.5 us: per_device(): got_diag = lax.ppermute(diag, ('row', 'col'), return_pairs_down)]
    slice x4 -> x0, local copies, waits for them, and re-layouts: 11.5 us -> none  [the longest x1 9 us: per_device(): right_side[first_row:first_row + row_step * BLOCK_SIZE]]
  transfers between devices with their start and end apart: 12 -> 2, of which waited for: 11 -> 1; matrix products, arithmetic and copies ran while one was open for 11% -> 0% of each run, Pallas kernels for 0% -> 0%
where the time goes in v1:
time: 342 us; the launch traced here: 341 us
  Pallas kernels  308 us (90%)
  waiting for transfers between devices  16.5 us (5%)
  local copies, waits for them, and re-layouts  11.6 us (3%)
    pallas_call x1, Pallas kernels, per_device(): pl.pallas_call(kernel, out_shape=(jax.ShapeDtypeStruct(grad_out.shape, bf...  308 us
    ppermute x1, waiting for transfers between devices, per_device(): got_diag = lax.ppermute(diag, ('row', 'col'), return_pairs_down)  16.5 us
    unnamed x7, local copies, waits for them, and re-layouts  11.6 us
  transfers between devices with their start and end apart: 2, of which 1 were waited for; matrix products, arithmetic and copies ran while one was open for 0% of the time, Pallas kernels for 0%

profile of v1, /device:TPU:0, one launch (start us, length us, event | category | flops | bytes accessed | tf_op | source)
XLA Modules:
  0.0 341.4 jit_solution(17190570873668823870)
XLA Ops:
  0.6 308.4 %shard_map.50 = (bf16[1536,4096]{1,0:T(8,128)(2,1)}, bf16[12,256,256]{2,1,0:T(8,128)(2,1)}, bf16[9,256,256]{2,1,0:T(8,128)(2,1)}, bf16[3,256,256]{2,1,0:T(8,128)(2,1)}) custom-call(bf16[1536,768]{1,0:T(8,128)(2,1)} %lower.1, bf16[1536,4096]{1,0:T(8,128)(2,1)} %right.1, bf16[1536,4096]{1,0:T(8,128)(2,1)} %grad.1), custom_call_target="tpu_custom_call" | custom-call | tf_op jit(solution)/shard_map/pallas_call | solution.py:288
  309.0 0.0 copy-start
  309.0 1.5 collective-permute-start.1
  310.5 1.3 collective-permute-start
  311.9 16.5 %collective-permute-done = bf16[3,256,256]{2,1,0:T(8,128)(2,1)S(1)} collective-permute-done((bf16[3,256,256]{2,1,0:T(8,128)(2,1)}, bf16[3,256,256]{2,1,0:T(8,128)(2,1)S(1)}, u32[]{:S(2)}, u32[]{:S(2)}) %collective-permute-start) | collective-permute-done | bytes 393248 | tf_op jit(solution)/shard_map/ppermute | solution.py:307
  328.4 1.1 fusion.3
  329.5 0.0 collective-permute-done.1
  329.5 0.0 copy-done
  329.5 0.1 fusion.2
  329.7 0.1 maximum_dynamic-update-slice_fusion.3
  329.7 0.1 maximum_dynamic-update-slice_fusion.2
  329.9 0.0 copy-start.1
  329.9 11.5 %copy.11 = bf16[1536,4096]{1,0:T(8,128)(2,1)} copy(bf16[1536,4096]{1,0:T(8,128)(2,1)} %get-tuple-element.24) | data formatting | bytes 25165824
  341.4 0.0 copy-done.1
  (6 shorter events, 0.1 us)
Async XLA Ops:
  309.0 20.5 %copy-start = (bf16[12,256,256]{2,1,0:T(8,128)(2,1)S(1)}, bf16[12,256,256]{2,1,0:T(8,128)(2,1)}, u32[]{:S(2)}) copy-start(bf16[12,256,256]{2,1,0:T(8,128)(2,1)} %get-tuple-element.7) | copy-start | bytes 4718596
  309.0 20.4 %collective-permute-start.1 = (bf16[9,256,256]{2,1,0:T(8,128)(2,1)}, bf16[9,256,256]{2,1,0:T(8,128)(2,1)S(1)}, u32[]{:S(2)}, u32[]{:S(2)}) collective-permute-start(bf16[9,256,256]{2,1,0:T(8,128)(2,1)} %get-tuple-element.9), channel_id=1, source_target_pairs={{0,4},{2,6},{5,1},{7,3}} | collective-permute-start | bytes 3538952 | tf_op jit(solution)/shard_map/ppermute | solution.py:306
  310.5 17.8 %collective-permute-start = (bf16[3,256,256]{2,1,0:T(8,128)(2,1)}, bf16[3,256,256]{2,1,0:T(8,128)(2,1)S(1)}, u32[]{:S(2)}, u32[]{:S(2)}) collective-permute-start(bf16[3,256,256]{2,1,0:T(8,128)(2,1)} %get-tuple-element.8), channel_id=1, source_target_pairs={{0,4},{2,6}} | collective-permute-start | bytes 1179656 | tf_op jit(solution)/shard_map/ppermute | solution.py:307
  329.9 11.5 %copy-start.1 = (bf16[1536,768]{1,0:T(8,128)(2,1)}, bf16[1536,768]{1,0:T(8,128)(2,1)S(1)}, u32[]{:S(2)}) copy-start(bf16[1536,768]{1,0:T(8,128)(2,1)S(1)} %maximum_dynamic-update-slice_fusion) | copy-start | bytes 7077892

commit v2 on v1

--- a/solution.py
+++ b/solution.py
@@ -16,18 +16,23 @@
 COMMON = {(1, 0): 0, (2, 0): 1, (3, 0): 2, (3, 1): 3, (4, 0): 4, (4, 1): 5, (5, 0): 6, (5, 1): 7, (5, 2): 8}
 
 
-def packed_row(p, m):
-    return (PANEL_START[p] + m - 2 * p) * BLOCK
+RETURNED = 6
+RETURNED_FROM = 5
+COPY_PARTS = 12
+
+
+def packed(p, m):
+    return PANEL_START[p] + m - 2 * p
 
 
 def dot_nt(lhs, rhs):
     return lax.dot_general(lhs, rhs, (((1,), (1,)), ((), ())), preferred_element_type=jnp.float32)
 
 
-def kernel(lower, right, grad, out_right, out_same, out_cross, out_diag,
+def kernel(lower, right, grad, out_right, out_same, out_cross, out_diag, out_back,
            grad_v, right_v, other_v, lower_v, slot, hop, fin_same, fin_cross, fin_diag, total, stage, turned,
            grad_send, grad_recv, load_sem, low_load, low_cross_send, low_cross_recv, low_send, low_recv,
-           core_send, core_recv, hop_send, hop_recv, out_sem, fin_sem, core_free, hop_free):
+           core_send, core_recv, hop_send, hop_recv, back_send, back_recv, out_sem, fin_sem, core_free, hop_free):
     row = lax.axis_index("row")
     col = lax.axis_index("col")
     x = col // 2
@@ -36,6 +41,7 @@
     to_row = {"row": 1 - row}
     to_core = {"col": col + 1 - 2 * (col % 2)}
     to_chip = {"col": lax.rem(col + 2, 4)}
+    to_diag = {"row": 1 - row, "col": col + 1 - 2 * (col % 2)}
 
     def remote(src, dst, send, recv, where):
         return pltpu.make_async_remote_copy(src_ref=src, dst_ref=dst, send_sem=send, recv_sem=recv, device_id=where, device_id_type=MESH)
@@ -43,14 +49,26 @@
     def send_grad(m):
         return remote(grad.at[pl.ds(m * BLOCK, BLOCK)], other_v.at[pl.ds(m * BLOCK, BLOCK)], grad_send.at[m], grad_recv.at[m], to_row)
 
-    def panel_src(p):
-        return lower.at[pl.ds(2 * p * BLOCK, (NUM - 2 * p) * BLOCK), pl.ds(p * BLOCK, BLOCK)]
-
-    def panel_dst(parity, p):
-        return lower_v.at[x, parity, pl.ds(PANEL_START[p] * BLOCK, (NUM - 2 * p) * BLOCK)]
-
-    def send_panel(p):
-        return remote(panel_src(p), panel_dst(1, p), low_cross_send.at[p], low_cross_recv.at[p], to_row)
+    def load_low(target, p, m):
+        return pltpu.make_async_copy(lower.at[pl.ds(m * BLOCK, BLOCK), pl.ds(p * BLOCK, BLOCK)], target.at[packed(p, m)], low_load.at[packed(p, m)])
+
+    def each_low(target, act):
+        for p in range(3):
+            for m in range(2 * p, NUM):
+                act(load_low(target, p, m))
+
+    def cross_near():
+        return remote(fin_same.at[pl.ds(0, 6)], lower_v.at[x, 1, pl.ds(0, 6)], low_cross_send.at[0], low_cross_recv.at[0], to_row)
+
+    def cross_hand():
+        return remote(fin_same.at[pl.ds(6, 6)], fin_cross.at[pl.ds(0, 6)], low_cross_send.at[1], low_cross_recv.at[1], to_core)
+
+    def cross_far():
+        return remote(fin_cross.at[pl.ds(0, 6)], lower_v.at[x, 1, pl.ds(6, 6)], low_cross_send.at[2], low_cross_recv.at[2], to_diag)
+
+    def send_back():
+        part = fin_cross.at[pl.ds(RETURNED, 9 - RETURNED)]
+        return remote(part, part, back_send, back_recv, to_row)
 
     def send_low(index, half, where):
         return remote(lower_v.at[half], lower_v.at[half], low_send.at[index], low_recv.at[index], where)
@@ -68,30 +86,41 @@
         return remote(slot.at[pl.ds(first, count)], hop.at[pl.ds(FINAL_START[m], count)], hop_send.at[group, m], hop_recv.at[group, m], to_chip)
 
     barrier = pltpu.get_barrier_semaphore()
-    for where in (to_row, to_core, to_chip):
+    for where in (to_row, to_core, to_chip, to_diag):
         pl.semaphore_signal(barrier, inc=1, device_id=where, device_id_type=MESH)
-    pl.semaphore_wait(barrier, 3)
-
-    @pl.when(guest)
-    def _():
-        for p in range(3):
-            send_panel(p).start()
-
-    for m in range(NUM - 1, 0, -1):
-        send_grad(m).start()
-
-    @pl.when(row == 1)
-    def _():
-        send_grad(0).start()
+    pl.semaphore_wait(barrier, 4)
+
+    send_grad(NUM - 1).start()
+
+    @pl.when(guest)
+    def _():
+        each_low(fin_same, lambda copy: copy.start())
+
+    @pl.when(owner)
+    def _():
+        each_low(lower_v.at[x, 0], lambda copy: copy.start())
 
     for m in range(NUM):
         load(grad, grad_v, m, 0).start()
         load(right, right_v, m, 1).start()
 
-    @pl.when(owner)
-    def _():
-        for p in range(3):
-            pltpu.make_async_copy(panel_src(p), panel_dst(0, p), low_load.at[p]).start()
+    @pl.when(guest)
+    def _():
+        each_low(fin_same, lambda copy: copy.wait())
+        cross_hand().start()
+        cross_near().start()
+
+    @pl.when(owner)
+    def _():
+        cross_hand().wait_recv()
+        cross_far().start()
+
+    for m in range(NUM - 2, 0, -1):
+        send_grad(m).start()
+
+    @pl.when(row == 1)
+    def _():
+        send_grad(0).start()
 
     def partial_sums(source, group, m):
         @pl.when(owner)
@@ -148,9 +177,9 @@
 
     @pl.when(owner)
     def _():
-        for p in range(3):
-            pltpu.make_async_copy(panel_src(p), panel_dst(0, p), low_load.at[p]).wait()
-            send_panel(p).wait_recv()
+        each_low(lower_v.at[x, 0], lambda copy: copy.wait())
+        cross_near().wait_recv()
+        cross_far().wait_recv()
         send_low(0, x, to_chip).start()
         send_low(1, x, to_core).start()
 
@@ -164,6 +193,7 @@
         send_low(0, 1 - x, to_chip).wait_recv()
         send_low(2, 1 - x, to_core).start()
         pl.semaphore_wait(hop_free, 1)
+        cross_far().wait_send()
 
     @pl.when(guest)
     def _():
@@ -177,7 +207,7 @@
         p, half = n // 2, n % 2
         for parity in range(2):
             for m in range(n, NUM):
-                turned[parity, :, pl.ds((m - n) * BLOCK, BLOCK)] = lower_v[half, parity, pl.ds(packed_row(p, m), BLOCK), :].T
+                turned[parity, :, pl.ds((m - n) * BLOCK, BLOCK)] = lower_v[half, parity, packed(p, m)].T
 
     def put(n):
         return pltpu.make_async_copy(stage, out_right.at[pl.ds(n * BLOCK, BLOCK)], out_sem)
@@ -205,6 +235,10 @@
         put(m).start()
         if m < NUM - 1:
             finish(1, m + 1)
+        if m + 1 == RETURNED_FROM:
+            @pl.when(owner)
+            def _():
+                send_back().start()
 
     turn(0)
 
@@ -241,11 +275,19 @@
     @pl.when(owner)
     def _():
         copies = [pltpu.make_async_copy(src, dst, fin_sem.at[k])
-                  for k, (src, dst) in enumerate(((fin_same, out_same), (fin_cross, out_cross), (fin_diag, out_diag)))]
+                  for k, (src, dst) in enumerate(((fin_same, out_same), (fin_cross.at[pl.ds(0, RETURNED)], out_cross), (fin_diag, out_diag)))]
         for copy in copies:
             copy.start()
         for copy in copies:
             copy.wait()
+        send_back().wait_send()
+
+    @pl.when(guest)
+    def _():
+        send_back().wait_recv()
+        copy = pltpu.make_async_copy(fin_cross.at[pl.ds(RETURNED, 9 - RETURNED)], out_back, fin_sem.at[0])
+        copy.start()
+        copy.wait()
 
     put(0).wait()
     for m in range(NUM - 1, 0, -1):
@@ -263,14 +305,28 @@
 
     @pl.when(guest)
     def _():
-        for p in range(3):
-            send_panel(p).wait_send()
+        cross_hand().wait_send()
+        cross_near().wait_send()
         for m in range(1, NUM):
             send_core(1, m).wait_send()
 
         @pl.when(row == 0)
         def _():
             send_core(1, 0).wait_send()
+
+
+def copy_kernel(source, target, buffer, read_sem, write_sem):
+    rows = source.shape[0] // COPY_PARTS
+    part = lambda ref, k: ref.at[pl.ds(k * rows, rows)]
+    reads = [pltpu.make_async_copy(part(source, k), part(buffer, k), read_sem.at[k]) for k in range(COPY_PARTS)]
+    writes = [pltpu.make_async_copy(part(buffer, k), part(target, k), write_sem.at[k]) for k in range(COPY_PARTS)]
+    for read in reads:
+        read.start()
+    for read, write in zip(reads, writes):
+        read.wait()
+        write.start()
+    for write in writes:
+        write.wait()
 
 
 def solution(mesh):
@@ -285,24 +341,32 @@
         dma = pltpu.SemaphoreType.DMA
         block = lambda count: jax.ShapeDtypeStruct((count, BLOCK, BLOCK), bf16)
         hbm = pl.BlockSpec(memory_space=pl.ANY)
-        grad_right, same, cross, diag = pl.pallas_call(
+        right_here, same, cross, diag, back = pl.pallas_call(
             kernel,
-            out_shape=(jax.ShapeDtypeStruct(grad_out.shape, bf16), block(12), block(9), block(3)),
+            out_shape=(jax.ShapeDtypeStruct(grad_out.shape, bf16), block(12), block(RETURNED), block(3), block(9 - RETURNED)),
             in_specs=[hbm] * 3,
-            out_specs=[hbm] * 4,
+            out_specs=[hbm] * 5,
             scratch_shapes=[
                 pltpu.VMEM((NUM * BLOCK, COLS), bf16), pltpu.VMEM((NUM * BLOCK, COLS), bf16), pltpu.VMEM((NUM * BLOCK, COLS), bf16),
-                pltpu.VMEM((2, 2, 12 * BLOCK, BLOCK), bf16),
+                pltpu.VMEM((2, 2, 12, BLOCK, BLOCK), bf16),
                 pltpu.VMEM((21, BLOCK, BLOCK), f32), pltpu.VMEM((12, BLOCK, BLOCK), f32),
                 pltpu.VMEM((12, BLOCK, BLOCK), bf16), pltpu.VMEM((9, BLOCK, BLOCK), bf16), pltpu.VMEM((3, BLOCK, BLOCK), bf16),
                 pltpu.VMEM((BLOCK, COLS), f32), pltpu.VMEM((BLOCK, COLS), bf16), pltpu.VMEM((2, BLOCK, NUM * BLOCK), bf16),
-                dma((NUM,)), dma((NUM,)), dma((2, NUM)), dma((3,)), dma((3,)), dma((3,)), dma((3,)), dma((3,)),
-                dma((2, NUM)), dma((2, NUM)), dma((2, NUM)), dma((2, NUM)), dma, dma((3,)),
+                dma((NUM,)), dma((NUM,)), dma((2, NUM)), dma((12,)), dma((3,)), dma((3,)), dma((3,)), dma((3,)),
+                dma((2, NUM)), dma((2, NUM)), dma((2, NUM)), dma((2, NUM)), dma, dma, dma, dma((3,)),
                 pltpu.SemaphoreType.REGULAR, pltpu.SemaphoreType.REGULAR,
             ],
             compiler_params=pltpu.CompilerParams(collective_id=1, has_side_effects=True, vmem_limit_bytes=VMEM_BYTES),
         )(lower_tri, right_side, grad_out)
 
+        grad_right = pl.pallas_call(
+            copy_kernel,
+            out_shape=jax.ShapeDtypeStruct(grad_out.shape, bf16),
+            in_specs=[hbm],
+            out_specs=hbm,
+            scratch_shapes=[pltpu.VMEM(grad_out.shape, bf16), dma((COPY_PARTS,)), dma((COPY_PARTS,))],
+            cost_estimate=pl.CostEstimate(flops=10 ** 10, bytes_accessed=4 * grad_out.size, transcendentals=0),
+        )(right_here)
         got = lax.ppermute(cross, ("row", "col"), return_pairs)
         got_diag = lax.ppermute(diag, ("row", "col"), return_pairs_down)
         row, col = lax.axis_index("row"), lax.axis_index("col")
@@ -312,7 +376,11 @@
         def piece(m, p):
             if p > m // 2:
                 return zero
-            moved = got[COMMON[m, p]] if (m, p) in COMMON else got_diag[m // 2]
+            place = COMMON.get((m, p))
+            if place is None:
+                moved = got_diag[m // 2]
+            else:
+                moved = got[place] if place < RETURNED else back[place - RETURNED]
             return jnp.where(is_owner, same[FINAL_START[m] + p], moved)
 
         grad_lower = jnp.concatenate([jnp.concatenate([piece(m, p) for p in range(3)], axis=1) for m in range(NUM)], axis=0)

time: 342 us -> 319 us (0.933)
  waiting for transfers between devices: 16.5 us -> 2.92 us
  local copies, waits for them, and re-layouts: 11.6 us -> 1.48 us
    ppermute x1, waiting for transfers between devices: 16.5 us -> 2.91 us  [per_device(): got_diag = lax.ppermute(diag, ('row', 'col'), return_pairs_down)]
    unnamed x7 -> x8, local copies, waits for them, and re-layouts: 11.6 us -> 1.46 us
    pallas_call x0 -> x1, Pallas kernels: none -> 9.33 us  [per_device(): pl.pallas_call(copy_kernel, out_shape=jax.ShapeDtypeStruct(grad_out.shape...]
    pallas_call x1, Pallas kernels: 308 us -> 302 us  [per_device(): pl.pallas_call(kernel, out_shape=(jax.ShapeDtypeStruct(grad_out.shape, bf...]
  transfers between devices with their start and end apart: 2 -> 2, of which waited for: 1 -> 1; matrix products, arithmetic and copies ran while one was open for 0% -> 0% of each run, Pallas kernels for 0% -> 3%
where the time goes in v2:
time: 319 us
  Pallas kernels  311 us (97%)
    pallas_call x1, Pallas kernels, per_device(): pl.pallas_call(kernel, out_shape=(jax.ShapeDtypeStruct(grad_out.shape, bf...  302 us
    pallas_call x1, Pallas kernels, per_device(): pl.pallas_call(copy_kernel, out_shape=jax.ShapeDtypeStruct(grad_out.shape...  9.33 us
  transfers between devices with their start and end apart: 2, of which 1 were waited for; matrix products, arithmetic and copies ran while one was open for 0% of the time, Pallas kernels for 3%

profile of v2, /device:TPU:0, one launch (start us, length us, event | category | flops | bytes accessed | tf_op | source)
XLA Modules:
  0.0 319.2 jit_solution(15198340293576909838)
XLA Ops:
  0.6 301.7 %shard_map.50 = (bf16[1536,4096]{1,0:T(8,128)(2,1)}, bf16[12,256,256]{2,1,0:T(8,128)(2,1)}, bf16[6,256,256]{2,1,0:T(8,128)(2,1)}, bf16[3,256,256]{2,1,0:T(8,128)(2,1)}, bf16[3,256,256]{2,1,0:T(8,128)(2,1)}) custom-call(bf16[1536,768]{1,0:T(8,128)(2,1)} %lower.1, bf16[1536,4096]{1,0:T(8,128)(2,1)} %right.1, bf16[1536,4096]{1,0:T(8,128)(2,1)} %grad.1), custom_call_target="tpu_custom_call" | custom-call | tf_op jit(solution)/shard_map/pallas_call | solution.py:344
  302.4 1.3 collective-permute-start.1
  303.7 1.3 collective-permute-start
  305.0 0.0 copy-start
  305.0 0.0 copy-start.1
  305.0 9.3 %shard_map.51 = bf16[1536,4096]{1,0:T(8,128)(2,1)} custom-call(bf16[1536,4096]{1,0:T(8,128)(2,1)} %get-tuple-element.7.source), custom_call_target="tpu_custom_call" | custom-call | flops 10000000000 | bytes 25165824 | tf_op jit(solution)/shard_map/pallas_call | solution.py:362
  314.4 2.9 collective-permute-done
  317.3 0.0 copy-done
  317.3 0.0 copy-done.1
  317.3 0.1 select_bitcast_fusion.2
  317.5 0.0 collective-permute-done.1
  317.5 0.1 fusion.2
  317.6 0.1 maximum_dynamic-update-slice_fusion.3
  317.7 0.1 maximum_dynamic-update-slice_fusion.2
  317.8 0.0 copy-start.2
  317.8 1.4 copy-done.2
  (6 shorter events, 0.1 us)
Async XLA Ops:
  302.4 15.1 %collective-permute-start.1 = (bf16[6,256,256]{2,1,0:T(8,128)(2,1)}, bf16[6,256,256]{2,1,0:T(8,128)(2,1)S(1)}, u32[]{:S(2)}, u32[]{:S(2)}) collective-permute-start(bf16[6,256,256]{2,1,0:T(8,128)(2,1)} %get-tuple-element.10), channel_id=1, source_target_pairs={{0,4},{2,6},{5,1},{7,3}} | collective-permute-start | bytes 2359304 | tf_op jit(solution)/shard_map/ppermute | solution.py:370
  303.7 13.6 %collective-permute-start = (bf16[3,256,256]{2,1,0:T(8,128)(2,1)}, bf16[3,256,256]{2,1,0:T(8,128)(2,1)S(1)}, u32[]{:S(2)}, u32[]{:S(2)}) collective-permute-start(bf16[3,256,256]{2,1,0:T(8,128)(2,1)} %get-tuple-element.9), channel_id=1, source_target_pairs={{0,4},{2,6}} | collective-permute-start | bytes 1179656 | tf_op jit(solution)/shard_map/ppermute | solution.py:371
  305.0 12.3 %copy-start = (bf16[12,256,256]{2,1,0:T(8,128)(2,1)S(1)}, bf16[12,256,256]{2,1,0:T(8,128)(2,1)}, u32[]{:S(2)}) copy-start(bf16[12,256,256]{2,1,0:T(8,128)(2,1)} %get-tuple-element.8) | copy-start | bytes 4718596
  305.0 12.3 %copy-start.1 = (bf16[3,256,256]{2,1,0:T(8,128)(2,1)S(1)}, bf16[3,256,256]{2,1,0:T(8,128)(2,1)}, u32[]{:S(2)}) copy-start(bf16[3,256,256]{2,1,0:T(8,128)(2,1)} %get-tuple-element.11) | copy-start | bytes 1179652
  317.8 1.4 copy-start.2

commit v3 on v2

--- a/solution.py
+++ b/solution.py
@@ -10,29 +10,23 @@
 NUM = 6
 COLS = 4096
 TILE = 512
+LAST = 1024
 VMEM_BYTES = 67043328
-PANEL_START = (0, 6, 10)
-FINAL_START = (0, 1, 2, 4, 6, 9)
-COMMON = {(1, 0): 0, (2, 0): 1, (3, 0): 2, (3, 1): 3, (4, 0): 4, (4, 1): 5, (5, 0): 6, (5, 1): 7, (5, 2): 8}
-
-
+HOP_START = (0, 1, 2, 4, 6, 9)
+PLACE = {(1, 0): 0, (2, 0): 1, (3, 0): 2, (3, 1): 3, (4, 0): 4, (4, 1): 5, (5, 0): 6, (5, 1): 7, (5, 2): 8, (0, 0): 9, (2, 1): 10, (4, 2): 11}
 RETURNED = 6
 RETURNED_FROM = 5
 COPY_PARTS = 12
 
 
-def packed(p, m):
-    return PANEL_START[p] + m - 2 * p
-
-
 def dot_nt(lhs, rhs):
     return lax.dot_general(lhs, rhs, (((1,), (1,)), ((), ())), preferred_element_type=jnp.float32)
 
 
-def kernel(lower, right, grad, out_right, out_same, out_cross, out_diag, out_back,
-           grad_v, right_v, other_v, lower_v, slot, hop, fin_same, fin_cross, fin_diag, total, stage, turned,
+def kernel(lower, right, grad, out_right, out_low, out_cross,
+           grad_v, right_v, other_v, lower_v, slot, hop, fin_same, fin_cross, total, stage, turned,
            grad_send, grad_recv, load_sem, low_load, low_cross_send, low_cross_recv, low_send, low_recv,
-           core_send, core_recv, hop_send, hop_recv, back_send, back_recv, out_sem, fin_sem, core_free, hop_free):
+           core_send, core_recv, hop_send, hop_recv, back_send, back_recv, corner_send, corner_recv, out_sem, last_sem, fin_sem, core_free, hop_free):
     row = lax.axis_index("row")
     col = lax.axis_index("col")
     x = col // 2
@@ -49,8 +43,11 @@
     def send_grad(m):
         return remote(grad.at[pl.ds(m * BLOCK, BLOCK)], other_v.at[pl.ds(m * BLOCK, BLOCK)], grad_send.at[m], grad_recv.at[m], to_row)
 
+    def send_right():
+        return remote(right.at[pl.ds(0, BLOCK)], other_v.at[pl.ds(0, BLOCK)], grad_send.at[0], grad_recv.at[0], to_row)
+
     def load_low(target, p, m):
-        return pltpu.make_async_copy(lower.at[pl.ds(m * BLOCK, BLOCK), pl.ds(p * BLOCK, BLOCK)], target.at[packed(p, m)], low_load.at[packed(p, m)])
+        return pltpu.make_async_copy(lower.at[pl.ds(m * BLOCK, BLOCK), pl.ds(p * BLOCK, BLOCK)], target.at[PLACE[m, p]], low_load.at[PLACE[m, p]])
 
     def each_low(target, act):
         for p in range(3):
@@ -63,12 +60,16 @@
     def cross_hand():
         return remote(fin_same.at[pl.ds(6, 6)], fin_cross.at[pl.ds(0, 6)], low_cross_send.at[1], low_cross_recv.at[1], to_core)
 
-    def cross_far():
-        return remote(fin_cross.at[pl.ds(0, 6)], lower_v.at[x, 1, pl.ds(6, 6)], low_cross_send.at[2], low_cross_recv.at[2], to_diag)
+    def cross_far(count):
+        return remote(fin_cross.at[pl.ds(0, count)], lower_v.at[x, 1, pl.ds(6, count)], low_cross_send.at[2], low_cross_recv.at[2], to_diag)
 
     def send_back():
         part = fin_cross.at[pl.ds(RETURNED, 9 - RETURNED)]
-        return remote(part, part, back_send, back_recv, to_row)
+        return remote(part, part, back_send.at[0], back_recv.at[0], to_row)
+
+    def send_back_down():
+        part = fin_cross.at[pl.ds(10, 2)]
+        return remote(part, part, back_send.at[1], back_recv.at[1], to_row)
 
     def send_low(index, half, where):
         return remote(lower_v.at[half], lower_v.at[half], low_send.at[index], low_recv.at[index], where)
@@ -83,7 +84,11 @@
     def send_hop(group, m, side):
         base = m * (m + 1) // 2
         first, count = (base + m // 2 + 1, (m + 1) // 2) if side == 0 else (base, m // 2 + 1)
-        return remote(slot.at[pl.ds(first, count)], hop.at[pl.ds(FINAL_START[m], count)], hop_send.at[group, m], hop_recv.at[group, m], to_chip)
+        return remote(slot.at[pl.ds(first, count)], hop.at[pl.ds(HOP_START[m], count)], hop_send.at[group, m], hop_recv.at[group, m], to_chip)
+
+    @pl.when(guest)
+    def _():
+        fin_cross[9:] = jnp.zeros((3, BLOCK, BLOCK), jnp.bfloat16)
 
     barrier = pltpu.get_barrier_semaphore()
     for where in (to_row, to_core, to_chip, to_diag):
@@ -113,10 +118,22 @@
     @pl.when(owner)
     def _():
         cross_hand().wait_recv()
-        cross_far().start()
+
+        @pl.when(row == 0)
+        def _():
+            cross_far(3).start()
+
+        @pl.when(row == 1)
+        def _():
+            lower_v[x, 1, 9:] = jnp.zeros((3, BLOCK, BLOCK), jnp.bfloat16)
+            cross_far(6).start()
 
     for m in range(NUM - 2, 0, -1):
         send_grad(m).start()
+
+    @pl.when(row == 0)
+    def _():
+        send_right().start()
 
     @pl.when(row == 1)
     def _():
@@ -155,20 +172,24 @@
                     send_hop(group, m, side).wait_send()
                 for p in range(m // 2 + 1):
                     n = 2 * p + side
-                    target, place = (fin_cross, COMMON[m, p]) if (m, p) in COMMON else (fin_diag, m // 2)
-                    if group == 0:
-                        target, place = fin_same, FINAL_START[m] + p
+                    target = fin_cross if group else fin_same
                     if n > m:
-                        target[place] = jnp.zeros((BLOCK, BLOCK), jnp.bfloat16)
+                        target[PLACE[m, p]] = jnp.zeros((BLOCK, BLOCK), jnp.bfloat16)
                         continue
-                    value = slot[m * (m + 1) // 2 + side * (m // 2 + 1) + p] + hop[FINAL_START[m] + p]
+                    value = slot[m * (m + 1) // 2 + side * (m // 2 + 1) + p] + hop[HOP_START[m] + p]
                     if n == m and group == 0:
                         rows = lax.broadcasted_iota(jnp.int32, (BLOCK, BLOCK), 0)
                         cols = lax.broadcasted_iota(jnp.int32, (BLOCK, BLOCK), 1)
                         value = jnp.where(rows >= cols, value, 0.0)
                     if n == m and group == 1:
                         value = jnp.where(row == 0, value, 0.0)
-                    target[place] = value.astype(jnp.bfloat16)
+                    target[PLACE[m, p]] = value.astype(jnp.bfloat16)
+
+    def put_low(first, count, source):
+        return pltpu.make_async_copy(source.at[pl.ds(first, count)], out_low.at[pl.ds(first, count)], fin_sem.at[0])
+
+    def put_cross():
+        return pltpu.make_async_copy(fin_cross.at[pl.ds(0, RETURNED)], out_cross, fin_sem.at[1])
 
     for m in range(NUM):
         load(grad, grad_v, m, 0).wait()
@@ -179,7 +200,15 @@
     def _():
         each_low(lower_v.at[x, 0], lambda copy: copy.wait())
         cross_near().wait_recv()
-        cross_far().wait_recv()
+
+        @pl.when(row == 0)
+        def _():
+            cross_far(6).wait_recv()
+
+        @pl.when(row == 1)
+        def _():
+            cross_far(3).wait_recv()
+
         send_low(0, x, to_chip).start()
         send_low(1, x, to_core).start()
 
@@ -193,7 +222,15 @@
         send_low(0, 1 - x, to_chip).wait_recv()
         send_low(2, 1 - x, to_core).start()
         pl.semaphore_wait(hop_free, 1)
-        cross_far().wait_send()
+        put_low(0, 12, fin_same).start()
+
+        @pl.when(row == 0)
+        def _():
+            cross_far(3).wait_send()
+
+        @pl.when(row == 1)
+        def _():
+            cross_far(6).wait_send()
 
     @pl.when(guest)
     def _():
@@ -207,7 +244,7 @@
         p, half = n // 2, n % 2
         for parity in range(2):
             for m in range(n, NUM):
-                turned[parity, :, pl.ds((m - n) * BLOCK, BLOCK)] = lower_v[half, parity, packed(p, m)].T
+                turned[parity, :, pl.ds((m - n) * BLOCK, BLOCK)] = lower_v[half, parity, PLACE[m, p]].T
 
     def put(n):
         return pltpu.make_async_copy(stage, out_right.at[pl.ds(n * BLOCK, BLOCK)], out_sem)
@@ -239,6 +276,10 @@
             @pl.when(owner)
             def _():
                 send_back().start()
+        if m == 1:
+            @pl.when(jnp.logical_and(owner, row == 0))
+            def _():
+                send_back_down().start()
 
     turn(0)
 
@@ -248,71 +289,99 @@
 
     tiles(all_but_last)
     finish(1, 1)
+
+    @pl.when(owner)
+    def _():
+        put_cross().start()
+
     put(1).wait()
 
+    def put_last(t):
+        cols = pl.ds(t * LAST, LAST)
+        return pltpu.make_async_copy(stage.at[:, cols], out_right.at[pl.ds(0, BLOCK), cols], last_sem.at[t])
+
     @pl.when(row == 0)
     def _():
         send_grad(0).wait_recv()
-        partial_sums(other_v, 1, 0)
-
-        def last(cols):
+        for t in range(COLS // LAST):
+            cols = pl.ds(t * LAST, LAST)
             value = jnp.dot(turned[1, :, :BLOCK], other_v[:BLOCK, cols], preferred_element_type=jnp.float32)
             stage[:, cols] = (total[:, cols] + value).astype(jnp.bfloat16)
-
-        tiles(last)
-        put(0).start()
-        finish(1, 0)
+            put_last(t).start()
+
+    def corner_core():
+        return remote(slot.at[0], hop.at[0], corner_send.at[0], corner_recv.at[0], to_core)
+
+    def corner_chip():
+        return remote(slot.at[0], hop.at[1], corner_send.at[1], corner_recv.at[1], to_chip)
 
     @pl.when(row == 1)
     def _():
-        def last(cols):
+        for t in range(COLS // LAST):
+            cols = pl.ds(t * LAST, LAST)
             stage[:, cols] = total[:, cols].astype(jnp.bfloat16)
-
-        tiles(last)
-        put(0).start()
-        fin_diag[0] = jnp.zeros((BLOCK, BLOCK), jnp.bfloat16)
-
-    @pl.when(owner)
-    def _():
-        copies = [pltpu.make_async_copy(src, dst, fin_sem.at[k])
-                  for k, (src, dst) in enumerate(((fin_same, out_same), (fin_cross.at[pl.ds(0, RETURNED)], out_cross), (fin_diag, out_diag)))]
-        for copy in copies:
-            copy.start()
-        for copy in copies:
-            copy.wait()
-        send_back().wait_send()
+            put_last(t).start()
+        send_right().wait_recv()
+        slot[0] = dot_nt(grad_v[:BLOCK, :], other_v[:BLOCK, :])
+
+        @pl.when(owner)
+        def _():
+            corner_core().start()
+            corner_core().wait_send()
+
+        @pl.when(jnp.logical_and(guest, x == 1))
+        def _():
+            corner_core().wait_recv()
+            slot[0] = slot[0] + hop[0]
+            corner_chip().start()
+            corner_chip().wait_send()
+
+        @pl.when(jnp.logical_and(guest, x == 0))
+        def _():
+            corner_core().wait_recv()
+            corner_chip().wait_recv()
+            fin_cross[9] = (slot[0] + hop[0] + hop[1]).astype(jnp.bfloat16)
 
     @pl.when(guest)
     def _():
         send_back().wait_recv()
-        copy = pltpu.make_async_copy(fin_cross.at[pl.ds(RETURNED, 9 - RETURNED)], out_back, fin_sem.at[0])
-        copy.start()
-        copy.wait()
-
-    put(0).wait()
-    for m in range(NUM - 1, 0, -1):
-        send_grad(m).wait_send()
-
-    @pl.when(row == 1)
-    def _():
-        send_grad(0).wait_send()
-
-    @pl.when(owner)
-    def _():
-        send_low(0, x, to_chip).wait_send()
-        send_low(1, x, to_core).wait_send()
-        send_low(2, 1 - x, to_core).wait_send()
-
-    @pl.when(guest)
-    def _():
+
+        @pl.when(row == 1)
+        def _():
+            send_back_down().wait_recv()
+
+        put_low(RETURNED, 12 - RETURNED, fin_cross).start()
+        put_low(RETURNED, 12 - RETURNED, fin_cross).wait()
         cross_hand().wait_send()
         cross_near().wait_send()
         for m in range(1, NUM):
             send_core(1, m).wait_send()
 
+    @pl.when(owner)
+    def _():
+        put_low(0, 12, fin_same).wait()
+        put_cross().wait()
+        send_low(0, x, to_chip).wait_send()
+        send_low(1, x, to_core).wait_send()
+        send_low(2, 1 - x, to_core).wait_send()
+        send_back().wait_send()
+
         @pl.when(row == 0)
         def _():
-            send_core(1, 0).wait_send()
+            send_back_down().wait_send()
+
+    for t in range(COLS // LAST):
+        put_last(t).wait()
+    for m in range(NUM - 1, 0, -1):
+        send_grad(m).wait_send()
+
+    @pl.when(row == 0)
+    def _():
+        send_right().wait_send()
+
+    @pl.when(row == 1)
+    def _():
+        send_grad(0).wait_send()
 
 
 def copy_kernel(source, target, buffer, read_sem, write_sem):
@@ -334,26 +403,25 @@
     device = lambda row, col: row * 4 + col
     owners = [(row, 2 * chip + row) for row in range(2) for chip in range(2)]
     return_pairs = [(device(row, col), device(1 - row, col)) for row, col in owners]
-    return_pairs_down = [(src, dst) for src, dst in return_pairs if src < 4]
 
     def per_device(lower_tri, right_side, grad_out):
         bf16, f32 = jnp.bfloat16, jnp.float32
         dma = pltpu.SemaphoreType.DMA
         block = lambda count: jax.ShapeDtypeStruct((count, BLOCK, BLOCK), bf16)
         hbm = pl.BlockSpec(memory_space=pl.ANY)
-        right_here, same, cross, diag, back = pl.pallas_call(
+        right_here, low, cross = pl.pallas_call(
             kernel,
-            out_shape=(jax.ShapeDtypeStruct(grad_out.shape, bf16), block(12), block(RETURNED), block(3), block(9 - RETURNED)),
+            out_shape=(jax.ShapeDtypeStruct(grad_out.shape, bf16), block(12), block(RETURNED)),
             in_specs=[hbm] * 3,
-            out_specs=[hbm] * 5,
+            out_specs=[hbm] * 3,
             scratch_shapes=[
                 pltpu.VMEM((NUM * BLOCK, COLS), bf16), pltpu.VMEM((NUM * BLOCK, COLS), bf16), pltpu.VMEM((NUM * BLOCK, COLS), bf16),
                 pltpu.VMEM((2, 2, 12, BLOCK, BLOCK), bf16),
                 pltpu.VMEM((21, BLOCK, BLOCK), f32), pltpu.VMEM((12, BLOCK, BLOCK), f32),
-                pltpu.VMEM((12, BLOCK, BLOCK), bf16), pltpu.VMEM((9, BLOCK, BLOCK), bf16), pltpu.VMEM((3, BLOCK, BLOCK), bf16),
+                pltpu.VMEM((12, BLOCK, BLOCK), bf16), pltpu.VMEM((12, BLOCK, BLOCK), bf16),
                 pltpu.VMEM((BLOCK, COLS), f32), pltpu.VMEM((BLOCK, COLS), bf16), pltpu.VMEM((2, BLOCK, NUM * BLOCK), bf16),
                 dma((NUM,)), dma((NUM,)), dma((2, NUM)), dma((12,)), dma((3,)), dma((3,)), dma((3,)), dma((3,)),
-                dma((2, NUM)), dma((2, NUM)), dma((2, NUM)), dma((2, NUM)), dma, dma, dma, dma((3,)),
+                dma((2, NUM)), dma((2, NUM)), dma((2, NUM)), dma((2, NUM)), dma((2,)), dma((2,)), dma((2,)), dma((2,)), dma, dma((COLS // LAST,)), dma((2,)),
                 pltpu.SemaphoreType.REGULAR, pltpu.SemaphoreType.REGULAR,
             ],
             compiler_params=pltpu.CompilerParams(collective_id=1, has_side_effects=True, vmem_limit_bytes=VMEM_BYTES),
@@ -368,7 +436,6 @@
             cost_estimate=pl.CostEstimate(flops=10 ** 10, bytes_accessed=4 * grad_out.size, transcendentals=0),
         )(right_here)
         got = lax.ppermute(cross, ("row", "col"), return_pairs)
-        got_diag = lax.ppermute(diag, ("row", "col"), return_pairs_down)
         row, col = lax.axis_index("row"), lax.axis_index("col")
         is_owner = (col % 2) == row
         zero = jnp.zeros((BLOCK, BLOCK), bf16)
@@ -376,12 +443,8 @@
         def piece(m, p):
             if p > m // 2:
                 return zero
-            place = COMMON.get((m, p))
-            if place is None:
-                moved = got_diag[m // 2]
-            else:
-                moved = got[place] if place < RETURNED else back[place - RETURNED]
-            return jnp.where(is_owner, same[FINAL_START[m] + p], moved)
+            place = PLACE[m, p]
+            return jnp.where(is_owner, low[place], got[place]) if place < RETURNED else low[place]
 
         grad_lower = jnp.concatenate([jnp.concatenate([piece(m, p) for p in range(3)], axis=1) for m in range(NUM)], axis=0)
         return grad_right, grad_lower

time: 319 us -> 316 us (level)
  Pallas kernels: 311 us -> 305 us
  starting transfers between devices: 2.65 us -> 8.39 us
    ppermute x1, starting transfers between devices: 1.34 us -> 8.39 us  [per_device(): got = lax.ppermute(cross, ('row', 'col'), return_pairs)]
    pallas_call x1, Pallas kernels: 302 us -> 296 us  [per_device(): pl.pallas_call(kernel, out_shape=(jax.ShapeDtypeStruct(grad_out.shape, bf...]
  transfers between devices with their start and end apart: 2 -> 1, of which waited for: 1 -> 1; matrix products, arithmetic and copies ran while one was open for 0% -> 0% of each run, Pallas kernels for 3% -> 3%
where the time goes in v3:
time: 316 us
  Pallas kernels  305 us (97%)
  starting transfers between devices  8.39 us (3%)
    pallas_call x1, Pallas kernels, per_device(): pl.pallas_call(kernel, out_shape=(jax.ShapeDtypeStruct(grad_out.shape, bf...  296 us
    pallas_call x1, Pallas kernels, per_device(): pl.pallas_call(copy_kernel, out_shape=jax.ShapeDtypeStruct(grad_out.shape...  9.31 us
    ppermute x1, starting transfers between devices, per_device(): got = lax.ppermute(cross, ('row', 'col'), return_pairs)  8.39 us
  transfers between devices with their start and end apart: 1, of which 1 were waited for; matrix products, arithmetic and copies ran while one was open for 0% of the time, Pallas kernels for 3%

profile of v3, /device:TPU:0, one launch (start us, length us, event | category | flops | bytes accessed | tf_op | source)
XLA Modules:
  0.0 315.9 jit_solution(16680037457197641303)
XLA Ops:
  0.6 295.6 %shard_map.50 = (bf16[1536,4096]{1,0:T(8,128)(2,1)}, bf16[12,256,256]{2,1,0:T(8,128)(2,1)}, bf16[6,256,256]{2,1,0:T(8,128)(2,1)}) custom-call(bf16[1536,768]{1,0:T(8,128)(2,1)} %lower.1, bf16[1536,4096]{1,0:T(8,128)(2,1)} %right.1, bf16[1536,4096]{1,0:T(8,128)(2,1)} %grad.1), custom_call_target="tpu_custom_call" | custom-call | tf_op jit(solution)/shard_map/pallas_call | solution.py:412
  296.3 8.4 %collective-permute-start = (bf16[6,256,256]{2,1,0:T(8,128)(2,1)}, bf16[6,256,256]{2,1,0:T(8,128)(2,1)S(1)}, u32[]{:S(2)}, u32[]{:S(2)}) collective-permute-start(bf16[6,256,256]{2,1,0:T(8,128)(2,1)} %get-tuple-element.7), channel_id=1, source_target_pairs={{0,4},{2,6},{5,1},{7,3}} | collective-permute-start | bytes 2359304 | tf_op jit(solution)/shard_map/ppermute | solution.py:438
  304.7 0.0 copy-start
  304.7 9.3 %shard_map.51 = bf16[1536,4096]{1,0:T(8,128)(2,1)} custom-call(bf16[1536,4096]{1,0:T(8,128)(2,1)} %get-tuple-element.5.source), custom_call_target="tpu_custom_call" | custom-call | flops 10000000000 | bytes 25165824 | tf_op jit(solution)/shard_map/pallas_call | solution.py:430
  314.0 0.1 collective-permute-done
  314.1 0.0 copy-done
  314.1 0.2 slice_bitcast_fusion.2
  314.3 0.1 maximum_dynamic-update-slice_fusion.3
  314.4 0.1 maximum_dynamic-update-slice_fusion.2
  314.5 0.0 copy-start.1
  314.5 1.4 copy-done.1
  (6 shorter events, 0.1 us)
Async XLA Ops:
  296.3 17.8 %collective-permute-start = (bf16[6,256,256]{2,1,0:T(8,128)(2,1)}, bf16[6,256,256]{2,1,0:T(8,128)(2,1)S(1)}, u32[]{:S(2)}, u32[]{:S(2)}) collective-permute-start(bf16[6,256,256]{2,1,0:T(8,128)(2,1)} %get-tuple-element.7), channel_id=1, source_target_pairs={{0,4},{2,6},{5,1},{7,3}} | collective-permute-start | bytes 2359304 | tf_op jit(solution)/shard_map/ppermute | solution.py:438
  304.7 9.4 %copy-start = (bf16[12,256,256]{2,1,0:T(8,128)(2,1)S(1)}, bf16[12,256,256]{2,1,0:T(8,128)(2,1)}, u32[]{:S(2)}) copy-start(bf16[12,256,256]{2,1,0:T(8,128)(2,1)} %get-tuple-element.6) | copy-start | bytes 4718596
  314.5 1.4 copy-start.1

commit v4 on v3

--- a/solution.py
+++ b/solution.py
@@ -11,6 +11,7 @@
 COLS = 4096
 TILE = 512
 LAST = 1024
+HALF = BLOCK // 2
 VMEM_BYTES = 67043328
 HOP_START = (0, 1, 2, 4, 6, 9)
 PLACE = {(1, 0): 0, (2, 0): 1, (3, 0): 2, (3, 1): 3, (4, 0): 4, (4, 1): 5, (5, 0): 6, (5, 1): 7, (5, 2): 8, (0, 0): 9, (2, 1): 10, (4, 2): 11}
@@ -25,8 +26,8 @@
 
 def kernel(lower, right, grad, out_right, out_low, out_cross,
            grad_v, right_v, other_v, lower_v, slot, hop, fin_same, fin_cross, total, stage, turned,
-           grad_send, grad_recv, load_sem, low_load, low_cross_send, low_cross_recv, low_send, low_recv,
-           core_send, core_recv, hop_send, hop_recv, back_send, back_recv, corner_send, corner_recv, out_sem, last_sem, fin_sem, core_free, hop_free):
+           grad_send, grad_recv, last_send, last_recv, right_send, right_recv, load_sem, low_load, low_cross_send, low_cross_recv, low_send, low_recv,
+           core_send, core_recv, hop_send, hop_recv, back_send, back_recv, corner_send, corner_recv, out_sem, put_sem, fin_sem, core_free, hop_free):
     row = lax.axis_index("row")
     col = lax.axis_index("col")
     x = col // 2
@@ -43,8 +44,13 @@
     def send_grad(m):
         return remote(grad.at[pl.ds(m * BLOCK, BLOCK)], other_v.at[pl.ds(m * BLOCK, BLOCK)], grad_send.at[m], grad_recv.at[m], to_row)
 
-    def send_right():
-        return remote(right.at[pl.ds(0, BLOCK)], other_v.at[pl.ds(0, BLOCK)], grad_send.at[0], grad_recv.at[0], to_row)
+    def send_last(t):
+        cols = pl.ds(t * LAST, LAST)
+        return remote(grad.at[pl.ds(0, BLOCK), cols], other_v.at[pl.ds(0, BLOCK), cols], last_send.at[t], last_recv.at[t], to_row)
+
+    def send_right(h):
+        rows = pl.ds(h * HALF, HALF)
+        return remote(right.at[rows], other_v.at[rows], right_send.at[h], right_recv.at[h], to_row)
 
     def load_low(target, p, m):
         return pltpu.make_async_copy(lower.at[pl.ds(m * BLOCK, BLOCK), pl.ds(p * BLOCK, BLOCK)], target.at[PLACE[m, p]], low_load.at[PLACE[m, p]])
@@ -64,18 +70,23 @@
         return remote(fin_cross.at[pl.ds(0, count)], lower_v.at[x, 1, pl.ds(6, count)], low_cross_send.at[2], low_cross_recv.at[2], to_diag)
 
     def send_back():
-        part = fin_cross.at[pl.ds(RETURNED, 9 - RETURNED)]
-        return remote(part, part, back_send.at[0], back_recv.at[0], to_row)
+        part = pl.ds(RETURNED, 9 - RETURNED)
+        return remote(fin_cross.at[part], out_low.at[part], back_send.at[0], back_recv.at[0], to_row)
 
     def send_back_down():
-        part = fin_cross.at[pl.ds(10, 2)]
-        return remote(part, part, back_send.at[1], back_recv.at[1], to_row)
+        return remote(fin_cross.at[pl.ds(10, 2)], out_low.at[pl.ds(10, 2)], back_send.at[1], back_recv.at[1], to_row)
 
     def send_low(index, half, where):
         return remote(lower_v.at[half], lower_v.at[half], low_send.at[index], low_recv.at[index], where)
 
     def load(src, dst, m, k):
         return pltpu.make_async_copy(src.at[pl.ds(m * BLOCK, BLOCK)], dst.at[pl.ds(m * BLOCK, BLOCK)], load_sem.at[k, m])
+
+    def put_low(first, count, source):
+        return pltpu.make_async_copy(source.at[pl.ds(first, count)], out_low.at[pl.ds(first, count)], fin_sem.at[0])
+
+    def put_cross():
+        return pltpu.make_async_copy(fin_cross.at[pl.ds(0, RETURNED)], out_cross, fin_sem.at[1])
 
     def send_core(group, m):
         part = slot.at[pl.ds(m * (m + 1) // 2, m + 1)]
@@ -128,16 +139,27 @@
             lower_v[x, 1, 9:] = jnp.zeros((3, BLOCK, BLOCK), jnp.bfloat16)
             cross_far(6).start()
 
-    for m in range(NUM - 2, 0, -1):
+    for m in range(NUM - 2, 1, -1):
         send_grad(m).start()
 
     @pl.when(row == 0)
     def _():
-        send_right().start()
+        send_right(0).start()
+
+    send_grad(1).start()
+
+    @pl.when(row == 0)
+    def _():
+        send_right(1).start()
 
     @pl.when(row == 1)
     def _():
-        send_grad(0).start()
+        for t in range(COLS // LAST):
+            send_last(t).start()
+
+    @pl.when(jnp.logical_and(guest, row == 0))
+    def _():
+        put_low(9, 3, fin_cross).start()
 
     def partial_sums(source, group, m):
         @pl.when(owner)
@@ -185,12 +207,6 @@
                         value = jnp.where(row == 0, value, 0.0)
                     target[PLACE[m, p]] = value.astype(jnp.bfloat16)
 
-    def put_low(first, count, source):
-        return pltpu.make_async_copy(source.at[pl.ds(first, count)], out_low.at[pl.ds(first, count)], fin_sem.at[0])
-
-    def put_cross():
-        return pltpu.make_async_copy(fin_cross.at[pl.ds(0, RETURNED)], out_cross, fin_sem.at[1])
-
     for m in range(NUM):
         load(grad, grad_v, m, 0).wait()
         load(right, right_v, m, 1).wait()
@@ -255,7 +271,36 @@
             return carry
         lax.fori_loop(0, COLS // TILE, one, 0)
 
+    def corner(h):
+        cols = pl.ds(h * HALF, HALF)
+        to_guest = lambda: remote(slot.at[0, :, cols], hop.at[0, :, cols], corner_send.at[0, h], corner_recv.at[0, h], to_core)
+        to_first = lambda: remote(slot.at[0, :, cols], hop.at[1, :, cols], corner_send.at[1, h], corner_recv.at[1, h], to_chip)
+        send_right(h).wait_recv()
+        slot[0, :, cols] = dot_nt(grad_v[:BLOCK, :], other_v[pl.ds(h * HALF, HALF), :])
+
+        @pl.when(owner)
+        def _():
+            to_guest().start()
+            to_guest().wait_send()
+
+        @pl.when(jnp.logical_and(guest, x == 1))
+        def _():
+            to_guest().wait_recv()
+            slot[0, :, cols] = slot[0, :, cols] + hop[0, :, cols]
+            to_first().start()
+            to_first().wait_send()
+
+        @pl.when(jnp.logical_and(guest, x == 0))
+        def _():
+            to_guest().wait_recv()
+            to_first().wait_recv()
+            fin_cross[9, :, cols] = (slot[0, :, cols] + hop[0, :, cols] + hop[1, :, cols]).astype(jnp.bfloat16)
+
     for m in range(NUM - 1, 0, -1):
+        if m == 1:
+            @pl.when(row == 1)
+            def _():
+                corner(0)
         send_grad(m).wait_recv()
         partial_sums(other_v, 1, m)
         turn(m)
@@ -298,22 +343,16 @@
 
     def put_last(t):
         cols = pl.ds(t * LAST, LAST)
-        return pltpu.make_async_copy(stage.at[:, cols], out_right.at[pl.ds(0, BLOCK), cols], last_sem.at[t])
+        return pltpu.make_async_copy(stage.at[:, cols], out_right.at[pl.ds(0, BLOCK), cols], put_sem.at[t])
 
     @pl.when(row == 0)
     def _():
-        send_grad(0).wait_recv()
         for t in range(COLS // LAST):
             cols = pl.ds(t * LAST, LAST)
+            send_last(t).wait_recv()
             value = jnp.dot(turned[1, :, :BLOCK], other_v[:BLOCK, cols], preferred_element_type=jnp.float32)
             stage[:, cols] = (total[:, cols] + value).astype(jnp.bfloat16)
             put_last(t).start()
-
-    def corner_core():
-        return remote(slot.at[0], hop.at[0], corner_send.at[0], corner_recv.at[0], to_core)
-
-    def corner_chip():
-        return remote(slot.at[0], hop.at[1], corner_send.at[1], corner_recv.at[1], to_chip)
 
     @pl.when(row == 1)
     def _():
@@ -321,37 +360,21 @@
             cols = pl.ds(t * LAST, LAST)
             stage[:, cols] = total[:, cols].astype(jnp.bfloat16)
             put_last(t).start()
-        send_right().wait_recv()
-        slot[0] = dot_nt(grad_v[:BLOCK, :], other_v[:BLOCK, :])
-
-        @pl.when(owner)
-        def _():
-            corner_core().start()
-            corner_core().wait_send()
-
-        @pl.when(jnp.logical_and(guest, x == 1))
-        def _():
-            corner_core().wait_recv()
-            slot[0] = slot[0] + hop[0]
-            corner_chip().start()
-            corner_chip().wait_send()
-
-        @pl.when(jnp.logical_and(guest, x == 0))
-        def _():
-            corner_core().wait_recv()
-            corner_chip().wait_recv()
-            fin_cross[9] = (slot[0] + hop[0] + hop[1]).astype(jnp.bfloat16)
+        corner(1)
 
     @pl.when(guest)
     def _():
+        @pl.when(row == 0)
+        def _():
+            put_low(9, 3, fin_cross).wait()
+
+        @pl.when(row == 1)
+        def _():
+            put_low(9, 1, fin_cross).start()
+            put_low(9, 1, fin_cross).wait()
+            send_back_down().wait_recv()
+
         send_back().wait_recv()
-
-        @pl.when(row == 1)
-        def _():
-            send_back_down().wait_recv()
-
-        put_low(RETURNED, 12 - RETURNED, fin_cross).start()
-        put_low(RETURNED, 12 - RETURNED, fin_cross).wait()
         cross_hand().wait_send()
         cross_near().wait_send()
         for m in range(1, NUM):
@@ -377,11 +400,13 @@
 
     @pl.when(row == 0)
     def _():
-        send_right().wait_send()
+        for h in range(2):
+            send_right(h).wait_send()
 
     @pl.when(row == 1)
     def _():
-        send_grad(0).wait_send()
+        for t in range(COLS // LAST):
+            send_last(t).wait_send()
 
 
 def copy_kernel(source, target, buffer, read_sem, write_sem):
@@ -420,8 +445,8 @@
                 pltpu.VMEM((21, BLOCK, BLOCK), f32), pltpu.VMEM((12, BLOCK, BLOCK), f32),
                 pltpu.VMEM((12, BLOCK, BLOCK), bf16), pltpu.VMEM((12, BLOCK, BLOCK), bf16),
                 pltpu.VMEM((BLOCK, COLS), f32), pltpu.VMEM((BLOCK, COLS), bf16), pltpu.VMEM((2, BLOCK, NUM * BLOCK), bf16),
-                dma((NUM,)), dma((NUM,)), dma((2, NUM)), dma((12,)), dma((3,)), dma((3,)), dma((3,)), dma((3,)),
-                dma((2, NUM)), dma((2, NUM)), dma((2, NUM)), dma((2, NUM)), dma((2,)), dma((2,)), dma((2,)), dma((2,)), dma, dma((COLS // LAST,)), dma((2,)),
+                dma((NUM,)), dma((NUM,)), dma((COLS // LAST,)), dma((COLS // LAST,)), dma((2,)), dma((2,)), dma((2, NUM)), dma((12,)), dma((3,)), dma((3,)), dma((3,)), dma((3,)),
+                dma((2, NUM)), dma((2, NUM)), dma((2, NUM)), dma((2, NUM)), dma((2,)), dma((2,)), dma((2, 2)), dma((2, 2)), dma, dma((COLS // LAST,)), dma((2,)),
                 pltpu.SemaphoreType.REGULAR, pltpu.SemaphoreType.REGULAR,
             ],
             compiler_params=pltpu.CompilerParams(collective_id=1, has_side_effects=True, vmem_limit_bytes=VMEM_BYTES),

time: 316 us -> 314 us (level)
  no operation moved by 1% of the time
where the time goes in v4:
time: 314 us
  Pallas kernels  305 us (97%)
  starting transfers between devices  7.17 us (2%)
    pallas_call x1, Pallas kernels, per_device(): pl.pallas_call(kernel, out_shape=(jax.ShapeDtypeStruct(grad_out.shape, bf...  295 us
    pallas_call x1, Pallas kernels, per_device(): pl.pallas_call(copy_kernel, out_shape=jax.ShapeDtypeStruct(grad_out.shape...  9.31 us
    ppermute x1, starting transfers between devices, per_device(): got = lax.ppermute(cross, ('row', 'col'), return_pairs)  7.17 us
  transfers between devices with their start and end apart: 1, of which 1 were waited for; matrix products, arithmetic and copies ran while one was open for 0% of the time, Pallas kernels for 3%

profile of v4, /device:TPU:0, one launch (start us, length us, event | category | flops | bytes accessed | tf_op | source)
XLA Modules:
  0.0 314.3 jit_solution(14209252524574471244)
XLA Ops:
  0.6 295.2 %shard_map.50 = (bf16[1536,4096]{1,0:T(8,128)(2,1)}, bf16[12,256,256]{2,1,0:T(8,128)(2,1)}, bf16[6,256,256]{2,1,0:T(8,128)(2,1)}) custom-call(bf16[1536,768]{1,0:T(8,128)(2,1)} %lower.1, bf16[1536,4096]{1,0:T(8,128)(2,1)} %right.1, bf16[1536,4096]{1,0:T(8,128)(2,1)} %grad.1), custom_call_target="tpu_custom_call" | custom-call | tf_op jit(solution)/shard_map/pallas_call | solution.py:437
  295.9 7.2 %collective-permute-start = (bf16[6,256,256]{2,1,0:T(8,128)(2,1)}, bf16[6,256,256]{2,1,0:T(8,128)(2,1)S(1)}, u32[]{:S(2)}, u32[]{:S(2)}) collective-permute-start(bf16[6,256,256]{2,1,0:T(8,128)(2,1)} %get-tuple-element.7), channel_id=1, source_target_pairs={{0,4},{2,6},{5,1},{7,3}} | collective-permute-start | bytes 2359304 | tf_op jit(solution)/shard_map/ppermute | solution.py:463
  303.1 0.0 copy-start
  303.1 9.3 %shard_map.51 = bf16[1536,4096]{1,0:T(8,128)(2,1)} custom-call(bf16[1536,4096]{1,0:T(8,128)(2,1)} %get-tuple-element.5.source), custom_call_target="tpu_custom_call" | custom-call | flops 10000000000 | bytes 25165824 | tf_op jit(solution)/shard_map/pallas_call | solution.py:455
  312.4 0.1 collective-permute-done
  312.5 0.0 copy-done
  312.5 0.2 slice_bitcast_fusion.2
  312.7 0.1 maximum_dynamic-update-slice_fusion.3
  312.8 0.1 maximum_dynamic-update-slice_fusion.2
  312.9 0.0 copy-start.1
  312.9 1.4 copy-done.1
  (6 shorter events, 0.1 us)
Async XLA Ops:
  295.9 16.6 %collective-permute-start = (bf16[6,256,256]{2,1,0:T(8,128)(2,1)}, bf16[6,256,256]{2,1,0:T(8,128)(2,1)S(1)}, u32[]{:S(2)}, u32[]{:S(2)}) collective-permute-start(bf16[6,256,256]{2,1,0:T(8,128)(2,1)} %get-tuple-element.7), channel_id=1, source_target_pairs={{0,4},{2,6},{5,1},{7,3}} | collective-permute-start | bytes 2359304 | tf_op jit(solution)/shard_map/ppermute | solution.py:463
  303.1 9.4 %copy-start = (bf16[12,256,256]{2,1,0:T(8,128)(2,1)S(1)}, bf16[12,256,256]{2,1,0:T(8,128)(2,1)}, u32[]{:S(2)}) copy-start(bf16[12,256,256]{2,1,0:T(8,128)(2,1)} %get-tuple-element.6) | copy-start | bytes 4718596
  312.9 1.4 copy-start.1

commit v5 on v4

--- a/solution.py
+++ b/solution.py
@@ -26,7 +26,7 @@
 
 def kernel(lower, right, grad, out_right, out_low, out_cross,
            grad_v, right_v, other_v, lower_v, slot, hop, fin_same, fin_cross, total, stage, turned,
-           grad_send, grad_recv, last_send, last_recv, right_send, right_recv, load_sem, low_load, low_cross_send, low_cross_recv, low_send, low_recv,
+           grad_send, grad_recv, last_send, last_recv, right_send, right_recv, detour_send, detour_recv, load_sem, low_load, low_cross_send, low_cross_recv, low_send, low_recv,
            core_send, core_recv, hop_send, hop_recv, back_send, back_recv, corner_send, corner_recv, out_sem, put_sem, fin_sem, core_free, hop_free):
     row = lax.axis_index("row")
     col = lax.axis_index("col")
@@ -48,9 +48,9 @@
         cols = pl.ds(t * LAST, LAST)
         return remote(grad.at[pl.ds(0, BLOCK), cols], other_v.at[pl.ds(0, BLOCK), cols], last_send.at[t], last_recv.at[t], to_row)
 
-    def send_right(h):
-        rows = pl.ds(h * HALF, HALF)
-        return remote(right.at[rows], other_v.at[rows], right_send.at[h], right_recv.at[h], to_row)
+    def send_right(k):
+        where = (pl.ds(0, HALF), slice(None)) if k == 0 else (pl.ds(HALF, HALF), pl.ds((k - 1) * LAST, LAST))
+        return remote(right.at[where], other_v.at[where], right_send.at[k], right_recv.at[k], to_row)
 
     def load_low(target, p, m):
         return pltpu.make_async_copy(lower.at[pl.ds(m * BLOCK, BLOCK), pl.ds(p * BLOCK, BLOCK)], target.at[PLACE[m, p]], low_load.at[PLACE[m, p]])
@@ -60,14 +60,29 @@
             for m in range(2 * p, NUM):
                 act(load_low(target, p, m))
 
-    def cross_near():
-        return remote(fin_same.at[pl.ds(0, 6)], lower_v.at[x, 1, pl.ds(0, 6)], low_cross_send.at[0], low_cross_recv.at[0], to_row)
+    def cross_near(count):
+        return remote(fin_same.at[pl.ds(0, count)], lower_v.at[x, 1, pl.ds(0, count)], low_cross_send.at[0], low_cross_recv.at[0], to_row)
 
     def cross_hand():
-        return remote(fin_same.at[pl.ds(6, 6)], fin_cross.at[pl.ds(0, 6)], low_cross_send.at[1], low_cross_recv.at[1], to_core)
-
-    def cross_far(count):
-        return remote(fin_cross.at[pl.ds(0, count)], lower_v.at[x, 1, pl.ds(6, count)], low_cross_send.at[2], low_cross_recv.at[2], to_diag)
+        return remote(fin_same.at[pl.ds(4, 8)], fin_cross.at[pl.ds(0, 8)], low_cross_send.at[1], low_cross_recv.at[1], to_core)
+
+    def cross_far(first, count):
+        return remote(fin_cross.at[pl.ds(first - 4, count)], lower_v.at[x, 1, pl.ds(first, count)], low_cross_send.at[2], low_cross_recv.at[2], to_diag)
+
+    def detour(k):
+        source, target, where = (
+            (fin_same.at[pl.ds(10, 2)], fin_cross.at[pl.ds(0, 2)], to_chip),
+            (fin_cross.at[pl.ds(0, 2)], turned.at[:, :, pl.ds(0, BLOCK)], to_row),
+            (turned.at[:, :, pl.ds(0, BLOCK)], lower_v.at[0, 1, pl.ds(10, 2)], to_chip))[k]
+        return remote(source, target, detour_send.at[k], detour_recv.at[k], where)
+
+    def cross_cases(sender_row, act):
+        for case, counts in ((sender_row == 0, (5, 5, 4)),
+                             (jnp.logical_and(sender_row == 1, x == 0), (5, 5, 5)),
+                             (jnp.logical_and(sender_row == 1, x == 1), (4, 4, 5))):
+            @pl.when(case)
+            def _(counts=counts):
+                act(*counts)
 
     def send_back():
         part = pl.ds(RETURNED, 9 - RETURNED)
@@ -124,20 +139,26 @@
     def _():
         each_low(fin_same, lambda copy: copy.wait())
         cross_hand().start()
-        cross_near().start()
+
+        @pl.when(jnp.logical_and(row == 1, x == 0))
+        def _():
+            detour(0).start()
+
+        cross_cases(row, lambda near, first, far: cross_near(near).start())
+
+        @pl.when(jnp.logical_and(row == 1, x == 1))
+        def _():
+            detour(0).wait_recv()
+            detour(1).start()
 
     @pl.when(owner)
     def _():
+        @pl.when(jnp.logical_or(row == 1, x == 1))
+        def _():
+            lower_v[x, 1, 9:] = jnp.zeros((3, BLOCK, BLOCK), jnp.bfloat16)
+
         cross_hand().wait_recv()
-
-        @pl.when(row == 0)
-        def _():
-            cross_far(3).start()
-
-        @pl.when(row == 1)
-        def _():
-            lower_v[x, 1, 9:] = jnp.zeros((3, BLOCK, BLOCK), jnp.bfloat16)
-            cross_far(6).start()
+        cross_cases(row, lambda near, first, far: cross_far(first, far).start())
 
     for m in range(NUM - 2, 1, -1):
         send_grad(m).start()
@@ -150,7 +171,8 @@
 
     @pl.when(row == 0)
     def _():
-        send_right(1).start()
+        for k in range(1, 1 + COLS // LAST):
+            send_right(k).start()
 
     @pl.when(row == 1)
     def _():
@@ -215,15 +237,20 @@
     @pl.when(owner)
     def _():
         each_low(lower_v.at[x, 0], lambda copy: copy.wait())
-        cross_near().wait_recv()
-
-        @pl.when(row == 0)
-        def _():
-            cross_far(6).wait_recv()
-
-        @pl.when(row == 1)
-        def _():
-            cross_far(3).wait_recv()
+        def arrived(near, first, far):
+            cross_near(near).wait_recv()
+            cross_far(first, far).wait_recv()
+
+        cross_cases(1 - row, arrived)
+
+        @pl.when(jnp.logical_and(row == 0, x == 1))
+        def _():
+            detour(1).wait_recv()
+            detour(2).start()
+
+        @pl.when(jnp.logical_and(row == 0, x == 0))
+        def _():
+            detour(2).wait_recv()
 
         send_low(0, x, to_chip).start()
         send_low(1, x, to_core).start()
@@ -240,13 +267,11 @@
         pl.semaphore_wait(hop_free, 1)
         put_low(0, 12, fin_same).start()
 
-        @pl.when(row == 0)
-        def _():
-            cross_far(3).wait_send()
-
-        @pl.when(row == 1)
-        def _():
-            cross_far(6).wait_send()
+        cross_cases(row, lambda near, first, far: cross_far(first, far).wait_send())
+
+        @pl.when(jnp.logical_and(row == 0, x == 1))
+        def _():
+            detour(2).wait_send()
 
     @pl.when(guest)
     def _():
@@ -275,8 +300,15 @@
         cols = pl.ds(h * HALF, HALF)
         to_guest = lambda: remote(slot.at[0, :, cols], hop.at[0, :, cols], corner_send.at[0, h], corner_recv.at[0, h], to_core)
         to_first = lambda: remote(slot.at[0, :, cols], hop.at[1, :, cols], corner_send.at[1, h], corner_recv.at[1, h], to_chip)
-        send_right(h).wait_recv()
-        slot[0, :, cols] = dot_nt(grad_v[:BLOCK, :], other_v[pl.ds(h * HALF, HALF), :])
+        if h == 0:
+            send_right(0).wait_recv()
+            slot[0, :, cols] = dot_nt(grad_v[:BLOCK, :], other_v[:HALF, :])
+        else:
+            for t in range(COLS // LAST):
+                send_right(1 + t).wait_recv()
+                some = pl.ds(t * LAST, LAST)
+                value = dot_nt(grad_v[:BLOCK, some], other_v[HALF:BLOCK, some])
+                slot[0, :, cols] = value if t == 0 else slot[0, :, cols] + value
 
         @pl.when(owner)
         def _():
@@ -376,7 +408,16 @@
 
         send_back().wait_recv()
         cross_hand().wait_send()
-        cross_near().wait_send()
+        cross_cases(row, lambda near, first, far: cross_near(near).wait_send())
+
+        @pl.when(jnp.logical_and(row == 1, x == 0))
+        def _():
+            detour(0).wait_send()
+
+        @pl.when(jnp.logical_and(row == 1, x == 1))
+        def _():
+            detour(1).wait_send()
+
         for m in range(1, NUM):
             send_core(1, m).wait_send()
 
@@ -400,8 +441,8 @@
 
     @pl.when(row == 0)
     def _():
-        for h in range(2):
-            send_right(h).wait_send()
+        for k in range(1 + COLS // LAST):
+            send_right(k).wait_send()
 
     @pl.when(row == 1)
     def _():
@@ -445,7 +486,7 @@
                 pltpu.VMEM((21, BLOCK, BLOCK), f32), pltpu.VMEM((12, BLOCK, BLOCK), f32),
                 pltpu.VMEM((12, BLOCK, BLOCK), bf16), pltpu.VMEM((12, BLOCK, BLOCK), bf16),
                 pltpu.VMEM((BLOCK, COLS), f32), pltpu.VMEM((BLOCK, COLS), bf16), pltpu.VMEM((2, BLOCK, NUM * BLOCK), bf16),
-                dma((NUM,)), dma((NUM,)), dma((COLS // LAST,)), dma((COLS // LAST,)), dma((2,)), dma((2,)), dma((2, NUM)), dma((12,)), dma((3,)), dma((3,)), dma((3,)), dma((3,)),
+                dma((NUM,)), dma((NUM,)), dma((COLS // LAST,)), dma((COLS // LAST,)), dma((1 + COLS // LAST,)), dma((1 + COLS // LAST,)), dma((3,)), dma((3,)), dma((2, NUM)), dma((12,)), dma((3,)), dma((3,)), dma((3,)), dma((3,)),
                 dma((2, NUM)), dma((2, NUM)), dma((2, NUM)), dma((2, NUM)), dma((2,)), dma((2,)), dma((2, 2)), dma((2, 2)), dma, dma((COLS // LAST,)), dma((2,)),
                 pltpu.SemaphoreType.REGULAR, pltpu.SemaphoreType.REGULAR,
             ],

time: 314 us -> 311 us (level)
  no operation moved by 1% of the time
where the time goes in v5:
time: 311 us
  Pallas kernels  304 us (98%)
  starting transfers between devices  4.89 us (2%)
    pallas_call x1, Pallas kernels, per_device(): pl.pallas_call(kernel, out_shape=(jax.ShapeDtypeStruct(grad_out.shape, bf...  295 us
    pallas_call x1, Pallas kernels, per_device(): pl.pallas_call(copy_kernel, out_shape=jax.ShapeDtypeStruct(grad_out.shape...  9.31 us
  transfers between devices with their start and end apart: 1, of which 1 were waited for; matrix products, arithmetic and copies ran while one was open for 0% of the time, Pallas kernels for 3%

profile of v5, /device:TPU:0, one launch (start us, length us, event | category | flops | bytes accessed | tf_op | source)
XLA Modules:
  0.0 311.3 jit_solution(13581968084646747808)
XLA Ops:
  0.6 294.5 %shard_map.50 = (bf16[1536,4096]{1,0:T(8,128)(2,1)}, bf16[12,256,256]{2,1,0:T(8,128)(2,1)}, bf16[6,256,256]{2,1,0:T(8,128)(2,1)}) custom-call(bf16[1536,768]{1,0:T(8,128)(2,1)} %lower.1, bf16[1536,4096]{1,0:T(8,128)(2,1)} %right.1, bf16[1536,4096]{1,0:T(8,128)(2,1)} %grad.1), custom_call_target="tpu_custom_call" | custom-call | tf_op jit(solution)/shard_map/pallas_call | solution.py:478
  295.1 4.9 %collective-permute-start = (bf16[6,256,256]{2,1,0:T(8,128)(2,1)}, bf16[6,256,256]{2,1,0:T(8,128)(2,1)S(1)}, u32[]{:S(2)}, u32[]{:S(2)}) collective-permute-start(bf16[6,256,256]{2,1,0:T(8,128)(2,1)} %get-tuple-element.7), channel_id=1, source_target_pairs={{0,4},{2,6},{5,1},{7,3}} | collective-permute-start | bytes 2359304 | tf_op jit(solution)/shard_map/ppermute | solution.py:504
  300.1 0.0 copy-start
  300.1 9.3 %shard_map.51 = bf16[1536,4096]{1,0:T(8,128)(2,1)} custom-call(bf16[1536,4096]{1,0:T(8,128)(2,1)} %get-tuple-element.5.source), custom_call_target="tpu_custom_call" | custom-call | flops 10000000000 | bytes 25165824 | tf_op jit(solution)/shard_map/pallas_call | solution.py:496
  309.4 0.1 collective-permute-done
  309.5 0.0 copy-done
  309.5 0.2 slice_bitcast_fusion.2
  309.7 0.1 maximum_dynamic-update-slice_fusion.3
  309.8 0.1 maximum_dynamic-update-slice_fusion.2
  309.9 0.0 copy-start.1
  309.9 1.4 copy-done.1
  (6 shorter events, 0.1 us)
Async XLA Ops:
  295.1 14.3 %collective-permute-start = (bf16[6,256,256]{2,1,0:T(8,128)(2,1)}, bf16[6,256,256]{2,1,0:T(8,128)(2,1)S(1)}, u32[]{:S(2)}, u32[]{:S(2)}) collective-permute-start(bf16[6,256,256]{2,1,0:T(8,128)(2,1)} %get-tuple-element.7), channel_id=1, source_target_pairs={{0,4},{2,6},{5,1},{7,3}} | collective-permute-start | bytes 2359304 | tf_op jit(solution)/shard_map/ppermute | solution.py:504
  300.1 9.4 %copy-start = (bf16[12,256,256]{2,1,0:T(8,128)(2,1)S(1)}, bf16[12,256,256]{2,1,0:T(8,128)(2,1)}, u32[]{:S(2)}) copy-start(bf16[12,256,256]{2,1,0:T(8,128)(2,1)} %get-tuple-element.6) | copy-start | bytes 4718596
  309.9 1.4 copy-start.1

commit v6 on v5

--- a/solution.py
+++ b/solution.py
@@ -11,7 +11,8 @@
 COLS = 4096
 TILE = 512
 LAST = 1024
-HALF = BLOCK // 2
+NEAR = (0, 1)
+FAR = (2, 3)
 VMEM_BYTES = 67043328
 HOP_START = (0, 1, 2, 4, 6, 9)
 PLACE = {(1, 0): 0, (2, 0): 1, (3, 0): 2, (3, 1): 3, (4, 0): 4, (4, 1): 5, (5, 0): 6, (5, 1): 7, (5, 2): 8, (0, 0): 9, (2, 1): 10, (4, 2): 11}
@@ -25,8 +26,8 @@
 
 
 def kernel(lower, right, grad, out_right, out_low, out_cross,
-           grad_v, right_v, other_v, lower_v, slot, hop, fin_same, fin_cross, total, stage, turned,
-           grad_send, grad_recv, last_send, last_recv, right_send, right_recv, detour_send, detour_recv, load_sem, low_load, low_cross_send, low_cross_recv, low_send, low_recv,
+           grad_v, right_v, other_v, lower_v, slot, hop, corner, fin_same, fin_cross, total, stage, turned,
+           grad_send, grad_recv, last_send, last_recv, detour_send, detour_recv, load_sem, low_load, low_cross_send, low_cross_recv, low_send, low_recv,
            core_send, core_recv, hop_send, hop_recv, back_send, back_recv, corner_send, corner_recv, out_sem, put_sem, fin_sem, core_free, hop_free):
     row = lax.axis_index("row")
     col = lax.axis_index("col")
@@ -48,9 +49,9 @@
         cols = pl.ds(t * LAST, LAST)
         return remote(grad.at[pl.ds(0, BLOCK), cols], other_v.at[pl.ds(0, BLOCK), cols], last_send.at[t], last_recv.at[t], to_row)
 
-    def send_right(k):
-        where = (pl.ds(0, HALF), slice(None)) if k == 0 else (pl.ds(HALF, HALF), pl.ds((k - 1) * LAST, LAST))
-        return remote(right.at[where], other_v.at[where], right_send.at[k], right_recv.at[k], to_row)
+    def send_right(t):
+        cols = pl.ds(t * LAST, LAST)
+        return remote(right.at[pl.ds(0, BLOCK), cols], other_v.at[pl.ds(0, BLOCK), cols], last_send.at[t], last_recv.at[t], to_row)
 
     def load_low(target, p, m):
         return pltpu.make_async_copy(lower.at[pl.ds(m * BLOCK, BLOCK), pl.ds(p * BLOCK, BLOCK)], target.at[PLACE[m, p]], low_load.at[PLACE[m, p]])
@@ -78,18 +79,15 @@
 
     def cross_cases(sender_row, act):
         for case, counts in ((sender_row == 0, (5, 5, 4)),
-                             (jnp.logical_and(sender_row == 1, x == 0), (5, 5, 5)),
+                             (jnp.logical_and(sender_row == 1, x == 0), (4, 4, 6)),
                              (jnp.logical_and(sender_row == 1, x == 1), (4, 4, 5))):
             @pl.when(case)
             def _(counts=counts):
                 act(*counts)
 
-    def send_back():
-        part = pl.ds(RETURNED, 9 - RETURNED)
-        return remote(fin_cross.at[part], out_low.at[part], back_send.at[0], back_recv.at[0], to_row)
-
-    def send_back_down():
-        return remote(fin_cross.at[pl.ds(10, 2)], out_low.at[pl.ds(10, 2)], back_send.at[1], back_recv.at[1], to_row)
+    def send_back(k):
+        part = (pl.ds(RETURNED, 9 - RETURNED), pl.ds(0, 9), pl.ds(10, 2))[k]
+        return remote(fin_cross.at[part], out_low.at[part], back_send.at[k], back_recv.at[k], to_row)
 
     def send_low(index, half, where):
         return remote(lower_v.at[half], lower_v.at[half], low_send.at[index], low_recv.at[index], where)
@@ -163,16 +161,12 @@
     for m in range(NUM - 2, 1, -1):
         send_grad(m).start()
 
+    send_grad(1).start()
+
     @pl.when(row == 0)
     def _():
-        send_right(0).start()
-
-    send_grad(1).start()
-
-    @pl.when(row == 0)
-    def _():
-        for k in range(1, 1 + COLS // LAST):
-            send_right(k).start()
+        for t in FAR:
+            send_right(t).start()
 
     @pl.when(row == 1)
     def _():
@@ -296,43 +290,46 @@
             return carry
         lax.fori_loop(0, COLS // TILE, one, 0)
 
-    def corner(h):
-        cols = pl.ds(h * HALF, HALF)
-        to_guest = lambda: remote(slot.at[0, :, cols], hop.at[0, :, cols], corner_send.at[0, h], corner_recv.at[0, h], to_core)
-        to_first = lambda: remote(slot.at[0, :, cols], hop.at[1, :, cols], corner_send.at[1, h], corner_recv.at[1, h], to_chip)
-        if h == 0:
-            send_right(0).wait_recv()
-            slot[0, :, cols] = dot_nt(grad_v[:BLOCK, :], other_v[:HALF, :])
-        else:
-            for t in range(COLS // LAST):
-                send_right(1 + t).wait_recv()
-                some = pl.ds(t * LAST, LAST)
-                value = dot_nt(grad_v[:BLOCK, some], other_v[HALF:BLOCK, some])
-                slot[0, :, cols] = value if t == 0 else slot[0, :, cols] + value
-
-        @pl.when(owner)
-        def _():
-            to_guest().start()
-            to_guest().wait_send()
-
-        @pl.when(jnp.logical_and(guest, x == 1))
-        def _():
-            to_guest().wait_recv()
-            slot[0, :, cols] = slot[0, :, cols] + hop[0, :, cols]
-            to_first().start()
-            to_first().wait_send()
-
-        @pl.when(jnp.logical_and(guest, x == 0))
-        def _():
-            to_guest().wait_recv()
-            to_first().wait_recv()
-            fin_cross[9, :, cols] = (slot[0, :, cols] + hop[0, :, cols] + hop[1, :, cols]).astype(jnp.bfloat16)
+    first_core = (col % 2) == 0
+
+    def corner_core():
+        return remote(slot.at[0], corner.at[0], corner_send.at[0], corner_recv.at[0], to_core)
+
+    def corner_chip():
+        return remote(slot.at[0], corner.at[1], corner_send.at[1], corner_recv.at[1], to_chip)
+
+    def corner_row():
+        return remote(slot.at[0], corner.at[2], corner_send.at[2], corner_recv.at[2], to_row)
+
+    def corner_start(grads, rights, pieces):
+        for t in pieces:
+            cols = pl.ds(t * LAST, LAST)
+            value = dot_nt(grads[:BLOCK, cols], rights[:BLOCK, cols])
+            slot[0] = value if t == pieces[0] else slot[0] + value
+
+        @pl.when(jnp.logical_not(first_core))
+        def _():
+            corner_core().start()
+
+        @pl.when(first_core)
+        def _():
+            corner_core().wait_recv()
+            slot[0] = slot[0] + corner[0]
+
+            @pl.when(x == 1)
+            def _():
+                corner_chip().start()
+
+    def corner_end():
+        @pl.when(jnp.logical_not(first_core))
+        def _():
+            corner_core().wait_send()
+
+        @pl.when(jnp.logical_and(first_core, x == 1))
+        def _():
+            corner_chip().wait_send()
 
     for m in range(NUM - 1, 0, -1):
-        if m == 1:
-            @pl.when(row == 1)
-            def _():
-                corner(0)
         send_grad(m).wait_recv()
         partial_sums(other_v, 1, m)
         turn(m)
@@ -350,13 +347,9 @@
         if m < NUM - 1:
             finish(1, m + 1)
         if m + 1 == RETURNED_FROM:
-            @pl.when(owner)
+            @pl.when(jnp.logical_and(owner, row == 1))
             def _():
-                send_back().start()
-        if m == 1:
-            @pl.when(jnp.logical_and(owner, row == 0))
-            def _():
-                send_back_down().start()
+                send_back(0).start()
 
     turn(0)
 
@@ -367,7 +360,12 @@
     tiles(all_but_last)
     finish(1, 1)
 
-    @pl.when(owner)
+    @pl.when(jnp.logical_and(owner, row == 0))
+    def _():
+        send_back(1).start()
+        send_back(2).start()
+
+    @pl.when(jnp.logical_and(owner, row == 1))
     def _():
         put_cross().start()
 
@@ -385,6 +383,21 @@
             value = jnp.dot(turned[1, :, :BLOCK], other_v[:BLOCK, cols], preferred_element_type=jnp.float32)
             stage[:, cols] = (total[:, cols] + value).astype(jnp.bfloat16)
             put_last(t).start()
+            if t == NEAR[-1]:
+                corner_start(other_v, right_v, NEAR)
+
+            if t == NEAR[-1] + 1:
+                @pl.when(jnp.logical_and(first_core, x == 0))
+                def _():
+                    corner_chip().wait_recv()
+                    slot[0] = slot[0] + corner[1]
+                    corner_row().start()
+
+        corner_end()
+
+        @pl.when(jnp.logical_and(first_core, x == 0))
+        def _():
+            corner_row().wait_send()
 
     @pl.when(row == 1)
     def _():
@@ -392,21 +405,32 @@
             cols = pl.ds(t * LAST, LAST)
             stage[:, cols] = total[:, cols].astype(jnp.bfloat16)
             put_last(t).start()
-        corner(1)
+        for t in FAR:
+            send_right(t).wait_recv()
+        corner_start(grad_v, other_v, FAR)
+        corner_end()
+
+        @pl.when(jnp.logical_and(first_core, x == 0))
+        def _():
+            corner_chip().wait_recv()
+            corner_row().wait_recv()
+            fin_cross[9] = (slot[0] + corner[1] + corner[2]).astype(jnp.bfloat16)
+
 
     @pl.when(guest)
     def _():
         @pl.when(row == 0)
         def _():
             put_low(9, 3, fin_cross).wait()
+            send_back(0).wait_recv()
 
         @pl.when(row == 1)
         def _():
             put_low(9, 1, fin_cross).start()
             put_low(9, 1, fin_cross).wait()
-            send_back_down().wait_recv()
-
-        send_back().wait_recv()
+            send_back(1).wait_recv()
+            send_back(2).wait_recv()
+
         cross_hand().wait_send()
         cross_cases(row, lambda near, first, far: cross_near(near).wait_send())
 
@@ -424,15 +448,19 @@
     @pl.when(owner)
     def _():
         put_low(0, 12, fin_same).wait()
-        put_cross().wait()
         send_low(0, x, to_chip).wait_send()
         send_low(1, x, to_core).wait_send()
         send_low(2, 1 - x, to_core).wait_send()
-        send_back().wait_send()
 
         @pl.when(row == 0)
         def _():
-            send_back_down().wait_send()
+            send_back(1).wait_send()
+            send_back(2).wait_send()
+
+        @pl.when(row == 1)
+        def _():
+            put_cross().wait()
+            send_back(0).wait_send()
 
     for t in range(COLS // LAST):
         put_last(t).wait()
@@ -441,8 +469,8 @@
 
     @pl.when(row == 0)
     def _():
-        for k in range(1 + COLS // LAST):
-            send_right(k).wait_send()
+        for t in FAR:
+            send_right(t).wait_send()
 
     @pl.when(row == 1)
     def _():
@@ -468,7 +496,7 @@
     block_spec = P(("batch", "row"), "col")
     device = lambda row, col: row * 4 + col
     owners = [(row, 2 * chip + row) for row in range(2) for chip in range(2)]
-    return_pairs = [(device(row, col), device(1 - row, col)) for row, col in owners]
+    return_pairs = [(device(row, col), device(1 - row, col)) for row, col in owners if row == 1]
 
     def per_device(lower_tri, right_side, grad_out):
         bf16, f32 = jnp.bfloat16, jnp.float32
@@ -483,11 +511,11 @@
             scratch_shapes=[
                 pltpu.VMEM((NUM * BLOCK, COLS), bf16), pltpu.VMEM((NUM * BLOCK, COLS), bf16), pltpu.VMEM((NUM * BLOCK, COLS), bf16),
                 pltpu.VMEM((2, 2, 12, BLOCK, BLOCK), bf16),
-                pltpu.VMEM((21, BLOCK, BLOCK), f32), pltpu.VMEM((12, BLOCK, BLOCK), f32),
+                pltpu.VMEM((21, BLOCK, BLOCK), f32), pltpu.VMEM((12, BLOCK, BLOCK), f32), pltpu.VMEM((3, BLOCK, BLOCK), f32),
                 pltpu.VMEM((12, BLOCK, BLOCK), bf16), pltpu.VMEM((12, BLOCK, BLOCK), bf16),
                 pltpu.VMEM((BLOCK, COLS), f32), pltpu.VMEM((BLOCK, COLS), bf16), pltpu.VMEM((2, BLOCK, NUM * BLOCK), bf16),
-                dma((NUM,)), dma((NUM,)), dma((COLS // LAST,)), dma((COLS // LAST,)), dma((1 + COLS // LAST,)), dma((1 + COLS // LAST,)), dma((3,)), dma((3,)), dma((2, NUM)), dma((12,)), dma((3,)), dma((3,)), dma((3,)), dma((3,)),
-                dma((2, NUM)), dma((2, NUM)), dma((2, NUM)), dma((2, NUM)), dma((2,)), dma((2,)), dma((2, 2)), dma((2, 2)), dma, dma((COLS // LAST,)), dma((2,)),
+                dma((NUM,)), dma((NUM,)), dma((COLS // LAST,)), dma((COLS // LAST,)), dma((3,)), dma((3,)), dma((2, NUM)), dma((12,)), dma((3,)), dma((3,)), dma((3,)), dma((3,)),
+                dma((2, NUM)), dma((2, NUM)), dma((2, NUM)), dma((2, NUM)), dma((3,)), dma((3,)), dma((3,)), dma((3,)), dma, dma((COLS // LAST,)), dma((2,)),
                 pltpu.SemaphoreType.REGULAR, pltpu.SemaphoreType.REGULAR,
             ],
             compiler_params=pltpu.CompilerParams(collective_id=1, has_side_effects=True, vmem_limit_bytes=VMEM_BYTES),
@@ -503,14 +531,14 @@
         )(right_here)
         got = lax.ppermute(cross, ("row", "col"), return_pairs)
         row, col = lax.axis_index("row"), lax.axis_index("col")
-        is_owner = (col % 2) == row
+        is_back = jnp.logical_and(col % 2 == 1, row == 0)
         zero = jnp.zeros((BLOCK, BLOCK), bf16)
 
         def piece(m, p):
             if p > m // 2:
                 return zero
             place = PLACE[m, p]
-            return jnp.where(is_owner, low[place], got[place]) if place < RETURNED else low[place]
+            return jnp.where(is_back, got[place], low[place]) if place < RETURNED else low[place]
 
         grad_lower = jnp.concatenate([jnp.concatenate([piece(m, p) for p in range(3)], axis=1) for m in range(NUM)], axis=0)
         return grad_right, grad_lower

time: 311 us -> 309 us (level)
  the two profiles are of different devices: /device:TPU:0 before, /device:TPU:3 now
where the time goes in v6:
time: 309 us
  Pallas kernels  303 us (98%)
    pallas_call x1, Pallas kernels, per_device(): pl.pallas_call(kernel, out_shape=(jax.ShapeDtypeStruct(grad_out.shape, bf...  294 us
    pallas_call x1, Pallas kernels, per_device(): pl.pallas_call(copy_kernel, out_shape=jax.ShapeDtypeStruct(grad_out.shape...  9.31 us
  transfers between devices with their start and end apart: 1, of which 1 were waited for; matrix products, arithmetic and copies ran while one was open for 0% of the time, Pallas kernels for 3%

profile of v6, /device:TPU:3, one launch (start us, length us, event | category | flops | bytes accessed | tf_op | source)
XLA Modules:
  0.0 308.7 jit_solution(2836808575669721057)
XLA Ops:
  0.6 293.5 %shard_map.50 = (bf16[1536,4096]{1,0:T(8,128)(2,1)}, bf16[12,256,256]{2,1,0:T(8,128)(2,1)}, bf16[6,256,256]{2,1,0:T(8,128)(2,1)}) custom-call(bf16[1536,768]{1,0:T(8,128)(2,1)} %lower.1, bf16[1536,4096]{1,0:T(8,128)(2,1)} %right.1, bf16[1536,4096]{1,0:T(8,128)(2,1)} %grad.1), custom_call_target="tpu_custom_call" | custom-call | tf_op jit(solution)/shard_map/pallas_call | solution.py:506
  294.2 1.3 collective-permute-start
  295.5 0.0 copy-start
  295.5 9.3 %shard_map.51 = bf16[1536,4096]{1,0:T(8,128)(2,1)} custom-call(bf16[1536,4096]{1,0:T(8,128)(2,1)} %get-tuple-element.5.source), custom_call_target="tpu_custom_call" | custom-call | flops 10000000000 | bytes 25165824 | tf_op jit(solution)/shard_map/pallas_call | solution.py:524
  304.8 2.1 collective-permute-done
  306.9 0.0 copy-done
  306.9 0.2 slice_bitcast_fusion.2
  307.1 0.1 maximum_dynamic-update-slice_fusion.3
  307.2 0.1 maximum_dynamic-update-slice_fusion.2
  307.3 0.0 copy-start.1
  307.3 1.4 copy-done.1
  (6 shorter events, 0.1 us)
Async XLA Ops:
  294.2 12.7 %collective-permute-start = (bf16[6,256,256]{2,1,0:T(8,128)(2,1)}, bf16[6,256,256]{2,1,0:T(8,128)(2,1)S(1)}, u32[]{:S(2)}, u32[]{:S(2)}) collective-permute-start(bf16[6,256,256]{2,1,0:T(8,128)(2,1)} %get-tuple-element.7), channel_id=1, source_target_pairs={{5,1},{7,3}} | collective-permute-start | bytes 2359304 | tf_op jit(solution)/shard_map/ppermute | solution.py:532
  295.5 11.4 %copy-start = (bf16[12,256,256]{2,1,0:T(8,128)(2,1)S(1)}, bf16[12,256,256]{2,1,0:T(8,128)(2,1)}, u32[]{:S(2)}) copy-start(bf16[12,256,256]{2,1,0:T(8,128)(2,1)} %get-tuple-element.6) | copy-start | bytes 4718596
  307.3 1.4 copy-start.1

commit v7 on v6

--- a/solution.py
+++ b/solution.py
@@ -72,22 +72,32 @@
 
     def detour(k):
         source, target, where = (
-            (fin_same.at[pl.ds(10, 2)], fin_cross.at[pl.ds(0, 2)], to_chip),
-            (fin_cross.at[pl.ds(0, 2)], turned.at[:, :, pl.ds(0, BLOCK)], to_row),
-            (turned.at[:, :, pl.ds(0, BLOCK)], lower_v.at[0, 1, pl.ds(10, 2)], to_chip))[k]
+            (fin_same.at[pl.ds(9, 3)], fin_cross.at[pl.ds(0, 3)], to_chip),
+            (fin_cross.at[pl.ds(0, 3)], fin_same.at[pl.ds(0, 3)], to_row),
+            (fin_same.at[pl.ds(0, 3)], lower_v.at[0, 1, pl.ds(9, 3)], to_chip))[k]
         return remote(source, target, detour_send.at[k], detour_recv.at[k], where)
 
     def cross_cases(sender_row, act):
         for case, counts in ((sender_row == 0, (5, 5, 4)),
-                             (jnp.logical_and(sender_row == 1, x == 0), (4, 4, 6)),
+                             (jnp.logical_and(sender_row == 1, x == 0), (4, 4, 5)),
                              (jnp.logical_and(sender_row == 1, x == 1), (4, 4, 5))):
             @pl.when(case)
             def _(counts=counts):
                 act(*counts)
 
     def send_back(k):
-        part = (pl.ds(RETURNED, 9 - RETURNED), pl.ds(0, 9), pl.ds(10, 2))[k]
+        part = (pl.ds(0, 9), pl.ds(10, 2), pl.ds(RETURNED, 3), pl.ds(0, 1), pl.ds(RETURNED, 2))[k]
         return remote(fin_cross.at[part], out_low.at[part], back_send.at[k], back_recv.at[k], to_row)
+
+    def back_cases(kind, act):
+        @pl.when(x == 0)
+        def _():
+            act(kind)
+
+        if kind == 2:
+            @pl.when(x == 1)
+            def _():
+                act(4)
 
     def send_low(index, half, where):
         return remote(lower_v.at[half], lower_v.at[half], low_send.at[index], low_recv.at[index], where)
@@ -98,8 +108,11 @@
     def put_low(first, count, source):
         return pltpu.make_async_copy(source.at[pl.ds(first, count)], out_low.at[pl.ds(first, count)], fin_sem.at[0])
 
+    def put_zero(place, k):
+        return pltpu.make_async_copy(fin_cross.at[pl.ds(9, 1)], out_low.at[pl.ds(place, 1)], fin_sem.at[k])
+
     def put_cross():
-        return pltpu.make_async_copy(fin_cross.at[pl.ds(0, RETURNED)], out_cross, fin_sem.at[1])
+        return pltpu.make_async_copy(fin_cross.at[pl.ds(1, RETURNED - 1)], out_cross, fin_sem.at[1])
 
     def send_core(group, m):
         part = slot.at[pl.ds(m * (m + 1) // 2, m + 1)]
@@ -176,6 +189,11 @@
     @pl.when(jnp.logical_and(guest, row == 0))
     def _():
         put_low(9, 3, fin_cross).start()
+
+        @pl.when(x == 1)
+        def _():
+            put_zero(0, 2).start()
+            put_zero(8, 3).start()
 
     def partial_sums(source, group, m):
         @pl.when(owner)
@@ -241,6 +259,7 @@
         def _():
             detour(1).wait_recv()
             detour(2).start()
+            detour(2).wait_send()
 
         @pl.when(jnp.logical_and(row == 0, x == 0))
         def _():
@@ -262,10 +281,6 @@
         put_low(0, 12, fin_same).start()
 
         cross_cases(row, lambda near, first, far: cross_far(first, far).wait_send())
-
-        @pl.when(jnp.logical_and(row == 0, x == 1))
-        def _():
-            detour(2).wait_send()
 
     @pl.when(guest)
     def _():
@@ -349,7 +364,7 @@
         if m + 1 == RETURNED_FROM:
             @pl.when(jnp.logical_and(owner, row == 1))
             def _():
-                send_back(0).start()
+                back_cases(2, lambda k: send_back(k).start())
 
     turn(0)
 
@@ -362,12 +377,13 @@
 
     @pl.when(jnp.logical_and(owner, row == 0))
     def _():
+        send_back(0).start()
         send_back(1).start()
-        send_back(2).start()
 
     @pl.when(jnp.logical_and(owner, row == 1))
     def _():
         put_cross().start()
+        back_cases(3, lambda k: send_back(k).start())
 
     put(1).wait()
 
@@ -422,14 +438,21 @@
         @pl.when(row == 0)
         def _():
             put_low(9, 3, fin_cross).wait()
-            send_back(0).wait_recv()
+
+            @pl.when(x == 1)
+            def _():
+                put_zero(0, 2).wait()
+                put_zero(8, 3).wait()
+
+            for kind in (2, 3):
+                back_cases(kind, lambda k: send_back(k).wait_recv())
 
         @pl.when(row == 1)
         def _():
             put_low(9, 1, fin_cross).start()
             put_low(9, 1, fin_cross).wait()
+            send_back(0).wait_recv()
             send_back(1).wait_recv()
-            send_back(2).wait_recv()
 
         cross_hand().wait_send()
         cross_cases(row, lambda near, first, far: cross_near(near).wait_send())
@@ -454,13 +477,14 @@
 
         @pl.when(row == 0)
         def _():
+            send_back(0).wait_send()
             send_back(1).wait_send()
-            send_back(2).wait_send()
 
         @pl.when(row == 1)
         def _():
             put_cross().wait()
-            send_back(0).wait_send()
+            for kind in (2, 3):
+                back_cases(kind, lambda k: send_back(k).wait_send())
 
     for t in range(COLS // LAST):
         put_last(t).wait()
@@ -505,7 +529,7 @@
         hbm = pl.BlockSpec(memory_space=pl.ANY)
         right_here, low, cross = pl.pallas_call(
             kernel,
-            out_shape=(jax.ShapeDtypeStruct(grad_out.shape, bf16), block(12), block(RETURNED)),
+            out_shape=(jax.ShapeDtypeStruct(grad_out.shape, bf16), block(12), block(RETURNED - 1)),
             in_specs=[hbm] * 3,
             out_specs=[hbm] * 3,
             scratch_shapes=[
@@ -515,7 +539,7 @@
                 pltpu.VMEM((12, BLOCK, BLOCK), bf16), pltpu.VMEM((12, BLOCK, BLOCK), bf16),
                 pltpu.VMEM((BLOCK, COLS), f32), pltpu.VMEM((BLOCK, COLS), bf16), pltpu.VMEM((2, BLOCK, NUM * BLOCK), bf16),
                 dma((NUM,)), dma((NUM,)), dma((COLS // LAST,)), dma((COLS // LAST,)), dma((3,)), dma((3,)), dma((2, NUM)), dma((12,)), dma((3,)), dma((3,)), dma((3,)), dma((3,)),
-                dma((2, NUM)), dma((2, NUM)), dma((2, NUM)), dma((2, NUM)), dma((3,)), dma((3,)), dma((3,)), dma((3,)), dma, dma((COLS // LAST,)), dma((2,)),
+                dma((2, NUM)), dma((2, NUM)), dma((2, NUM)), dma((2, NUM)), dma((5,)), dma((5,)), dma((3,)), dma((3,)), dma, dma((COLS // LAST,)), dma((4,)),
                 pltpu.SemaphoreType.REGULAR, pltpu.SemaphoreType.REGULAR,
             ],
             compiler_params=pltpu.CompilerParams(collective_id=1, has_side_effects=True, vmem_limit_bytes=VMEM_BYTES),
@@ -538,7 +562,7 @@
             if p > m // 2:
                 return zero
             place = PLACE[m, p]
-            return jnp.where(is_back, got[place], low[place]) if place < RETURNED else low[place]
+            return jnp.where(is_back, got[place - 1], low[place]) if 0 < place < RETURNED else low[place]
 
         grad_lower = jnp.concatenate([jnp.concatenate([piece(m, p) for p in range(3)], axis=1) for m in range(NUM)], axis=0)
         return grad_right, grad_lower

time: 309 us -> 307 us (level)
  the two profiles are of different devices: /device:TPU:3 before, /device:TPU:0 now
where the time goes in v7:
time: 307 us; the launch traced here: 302 us
  Pallas kernels  299 us (97%)
    pallas_call x1, Pallas kernels, per_device(): pl.pallas_call(kernel, out_shape=(jax.ShapeDtypeStruct(grad_out.shape, bf...  290 us
    pallas_call x1, Pallas kernels, per_device(): pl.pallas_call(copy_kernel, out_shape=jax.ShapeDtypeStruct(grad_out.shape...  9.31 us
  transfers between devices with their start and end apart: 1, of which 0 were waited for; matrix products, arithmetic and copies ran while one was open for 0% of the time, Pallas kernels for 3%

profile of v7, /device:TPU:0, one launch (start us, length us, event | category | flops | bytes accessed | tf_op | source)
XLA Modules:
  0.0 302.4 jit_solution(10892592418185668460)
XLA Ops:
  0.6 289.8 %shard_map.50 = (bf16[1536,4096]{1,0:T(8,128)(2,1)}, bf16[12,256,256]{2,1,0:T(8,128)(2,1)}, bf16[5,256,256]{2,1,0:T(8,128)(2,1)}) custom-call(bf16[1536,768]{1,0:T(8,128)(2,1)} %lower.1, bf16[1536,4096]{1,0:T(8,128)(2,1)} %right.1, bf16[1536,4096]{1,0:T(8,128)(2,1)} %grad.1), custom_call_target="tpu_custom_call" | custom-call | tf_op jit(solution)/shard_map/pallas_call | solution.py:530
  290.4 0.7 collective-permute-start
  291.2 0.0 copy-start
  291.2 9.3 %shard_map.51 = bf16[1536,4096]{1,0:T(8,128)(2,1)} custom-call(bf16[1536,4096]{1,0:T(8,128)(2,1)} %get-tuple-element.5.source), custom_call_target="tpu_custom_call" | custom-call | flops 10000000000 | bytes 25165824 | tf_op jit(solution)/shard_map/pallas_call | solution.py:548
  300.5 0.0 collective-permute-done
  300.5 0.0 copy-done
  300.5 0.2 slice_bitcast_fusion.2
  300.8 0.1 maximum_dynamic-update-slice_fusion.3
  300.8 0.1 maximum_dynamic-update-slice_fusion.2
  301.0 0.0 copy-start.1
  301.0 1.4 copy-done.1
  (6 shorter events, 0.1 us)
Async XLA Ops:
  290.4 10.1 %collective-permute-start = (bf16[5,256,256]{2,1,0:T(8,128)(2,1)}, bf16[5,256,256]{2,1,0:T(8,128)(2,1)S(1)}, u32[]{:S(2)}, u32[]{:S(2)}) collective-permute-start(bf16[5,256,256]{2,1,0:T(8,128)(2,1)} %get-tuple-element.7), channel_id=1, source_target_pairs={{5,1},{7,3}} | collective-permute-start | bytes 1966088 | tf_op jit(solution)/shard_map/ppermute | solution.py:556
  291.2 9.3 %copy-start = (bf16[12,256,256]{2,1,0:T(8,128)(2,1)S(1)}, bf16[12,256,256]{2,1,0:T(8,128)(2,1)}, u32[]{:S(2)}) copy-start(bf16[12,256,256]{2,1,0:T(8,128)(2,1)} %get-tuple-element.6) | copy-start | bytes 4718596
  301.0 1.4 copy-start.1

commit v8 on v7

--- a/solution.py
+++ b/solution.py
@@ -17,6 +17,7 @@
 HOP_START = (0, 1, 2, 4, 6, 9)
 PLACE = {(1, 0): 0, (2, 0): 1, (3, 0): 2, (3, 1): 3, (4, 0): 4, (4, 1): 5, (5, 0): 6, (5, 1): 7, (5, 2): 8, (0, 0): 9, (2, 1): 10, (4, 2): 11}
 RETURNED = 6
+SPARE = (0, 3)
 RETURNED_FROM = 5
 COPY_PARTS = 12
 
@@ -65,10 +66,10 @@
         return remote(fin_same.at[pl.ds(0, count)], lower_v.at[x, 1, pl.ds(0, count)], low_cross_send.at[0], low_cross_recv.at[0], to_row)
 
     def cross_hand():
-        return remote(fin_same.at[pl.ds(4, 8)], fin_cross.at[pl.ds(0, 8)], low_cross_send.at[1], low_cross_recv.at[1], to_core)
+        return remote(fin_same.at[pl.ds(3, 9)], fin_cross.at[pl.ds(0, 9)], low_cross_send.at[1], low_cross_recv.at[1], to_core)
 
     def cross_far(first, count):
-        return remote(fin_cross.at[pl.ds(first - 4, count)], lower_v.at[x, 1, pl.ds(first, count)], low_cross_send.at[2], low_cross_recv.at[2], to_diag)
+        return remote(fin_cross.at[pl.ds(first - 3, count)], lower_v.at[x, 1, pl.ds(first, count)], low_cross_send.at[2], low_cross_recv.at[2], to_diag)
 
     def detour(k):
         source, target, where = (
@@ -80,24 +81,14 @@
     def cross_cases(sender_row, act):
         for case, counts in ((sender_row == 0, (5, 5, 4)),
                              (jnp.logical_and(sender_row == 1, x == 0), (4, 4, 5)),
-                             (jnp.logical_and(sender_row == 1, x == 1), (4, 4, 5))):
+                             (jnp.logical_and(sender_row == 1, x == 1), (3, 3, 6))):
             @pl.when(case)
             def _(counts=counts):
                 act(*counts)
 
     def send_back(k):
-        part = (pl.ds(0, 9), pl.ds(10, 2), pl.ds(RETURNED, 3), pl.ds(0, 1), pl.ds(RETURNED, 2))[k]
+        part = (pl.ds(0, 9), pl.ds(10, 2), pl.ds(RETURNED, 3))[k]
         return remote(fin_cross.at[part], out_low.at[part], back_send.at[k], back_recv.at[k], to_row)
-
-    def back_cases(kind, act):
-        @pl.when(x == 0)
-        def _():
-            act(kind)
-
-        if kind == 2:
-            @pl.when(x == 1)
-            def _():
-                act(4)
 
     def send_low(index, half, where):
         return remote(lower_v.at[half], lower_v.at[half], low_send.at[index], low_recv.at[index], where)
@@ -108,11 +99,23 @@
     def put_low(first, count, source):
         return pltpu.make_async_copy(source.at[pl.ds(first, count)], out_low.at[pl.ds(first, count)], fin_sem.at[0])
 
-    def put_zero(place, k):
-        return pltpu.make_async_copy(fin_cross.at[pl.ds(9, 1)], out_low.at[pl.ds(place, 1)], fin_sem.at[k])
-
-    def put_cross():
-        return pltpu.make_async_copy(fin_cross.at[pl.ds(1, RETURNED - 1)], out_cross, fin_sem.at[1])
+    def put_zero():
+        return pltpu.make_async_copy(fin_cross.at[pl.ds(9, 1)], out_low.at[pl.ds(8, 1)], fin_sem.at[1])
+
+    def put_cross(act):
+        def part(first, count, place, k):
+            return pltpu.make_async_copy(fin_cross.at[pl.ds(first, count)], out_cross.at[pl.ds(place, count)], fin_sem.at[k])
+
+        @pl.when(x == 0)
+        def _():
+            act(part(0, RETURNED, 0, 1))
+
+        @pl.when(x == 1)
+        def _():
+            act(part(RETURNED, 1, 0, 1))
+            act(part(1, 2, 1, 2))
+            act(part(RETURNED + 1, 1, 3, 3))
+            act(part(4, 2, 4, 4))
 
     def send_core(group, m):
         part = slot.at[pl.ds(m * (m + 1) // 2, m + 1)]
@@ -192,8 +195,7 @@
 
         @pl.when(x == 1)
         def _():
-            put_zero(0, 2).start()
-            put_zero(8, 3).start()
+            put_zero().start()
 
     def partial_sums(source, group, m):
         @pl.when(owner)
@@ -362,9 +364,9 @@
         if m < NUM - 1:
             finish(1, m + 1)
         if m + 1 == RETURNED_FROM:
-            @pl.when(jnp.logical_and(owner, row == 1))
+            @pl.when(jnp.logical_and(owner, jnp.logical_and(row == 1, x == 0)))
             def _():
-                back_cases(2, lambda k: send_back(k).start())
+                send_back(2).start()
 
     turn(0)
 
@@ -382,8 +384,7 @@
 
     @pl.when(jnp.logical_and(owner, row == 1))
     def _():
-        put_cross().start()
-        back_cases(3, lambda k: send_back(k).start())
+        put_cross(lambda copy: copy.start())
 
     put(1).wait()
 
@@ -439,13 +440,13 @@
         def _():
             put_low(9, 3, fin_cross).wait()
 
+            @pl.when(x == 0)
+            def _():
+                send_back(2).wait_recv()
+
             @pl.when(x == 1)
             def _():
-                put_zero(0, 2).wait()
-                put_zero(8, 3).wait()
-
-            for kind in (2, 3):
-                back_cases(kind, lambda k: send_back(k).wait_recv())
+                put_zero().wait()
 
         @pl.when(row == 1)
         def _():
@@ -482,9 +483,11 @@
 
         @pl.when(row == 1)
         def _():
-            put_cross().wait()
-            for kind in (2, 3):
-                back_cases(kind, lambda k: send_back(k).wait_send())
+            put_cross(lambda copy: copy.wait())
+
+            @pl.when(x == 0)
+            def _():
+                send_back(2).wait_send()
 
     for t in range(COLS // LAST):
         put_last(t).wait()
@@ -529,7 +532,7 @@
         hbm = pl.BlockSpec(memory_space=pl.ANY)
         right_here, low, cross = pl.pallas_call(
             kernel,
-            out_shape=(jax.ShapeDtypeStruct(grad_out.shape, bf16), block(12), block(RETURNED - 1)),
+            out_shape=(jax.ShapeDtypeStruct(grad_out.shape, bf16), block(12), block(RETURNED)),
             in_specs=[hbm] * 3,
             out_specs=[hbm] * 3,
             scratch_shapes=[
@@ -539,7 +542,7 @@
                 pltpu.VMEM((12, BLOCK, BLOCK), bf16), pltpu.VMEM((12, BLOCK, BLOCK), bf16),
                 pltpu.VMEM((BLOCK, COLS), f32), pltpu.VMEM((BLOCK, COLS), bf16), pltpu.VMEM((2, BLOCK, NUM * BLOCK), bf16),
                 dma((NUM,)), dma((NUM,)), dma((COLS // LAST,)), dma((COLS // LAST,)), dma((3,)), dma((3,)), dma((2, NUM)), dma((12,)), dma((3,)), dma((3,)), dma((3,)), dma((3,)),
-                dma((2, NUM)), dma((2, NUM)), dma((2, NUM)), dma((2, NUM)), dma((5,)), dma((5,)), dma((3,)), dma((3,)), dma, dma((COLS // LAST,)), dma((4,)),
+                dma((2, NUM)), dma((2, NUM)), dma((2, NUM)), dma((2, NUM)), dma((3,)), dma((3,)), dma((3,)), dma((3,)), dma, dma((COLS // LAST,)), dma((5,)),
                 pltpu.SemaphoreType.REGULAR, pltpu.SemaphoreType.REGULAR,
             ],
             compiler_params=pltpu.CompilerParams(collective_id=1, has_side_effects=True, vmem_limit_bytes=VMEM_BYTES),
@@ -556,14 +559,14 @@
         got = lax.ppermute(cross, ("row", "col"), return_pairs)
         row, col = lax.axis_index("row"), lax.axis_index("col")
         is_back = jnp.logical_and(col % 2 == 1, row == 0)
+        swapped = jnp.logical_and(is_back, col // 2 == 1)
         zero = jnp.zeros((BLOCK, BLOCK), bf16)
-
-        def piece(m, p):
-            if p > m // 2:
-                return zero
-            place = PLACE[m, p]
-            return jnp.where(is_back, got[place - 1], low[place]) if 0 < place < RETURNED else low[place]
-
+        got = jnp.where(is_back, got, low[:RETURNED])
+        spare = [jnp.where(swapped, zero, got[place]) for place in SPARE]
+        moved = [jnp.where(swapped, got[place], low[RETURNED + k]) for k, place in enumerate(SPARE)]
+        got, spare, moved = lax.optimization_barrier((got, spare, moved))
+        blocks = [spare[0], got[1], got[2], spare[1], got[4], got[5], moved[0], moved[1]] + [low[k] for k in range(8, 12)]
+        piece = lambda m, p: blocks[PLACE[m, p]] if p <= m // 2 else zero
         grad_lower = jnp.concatenate([jnp.concatenate([piece(m, p) for p in range(3)], axis=1) for m in range(NUM)], axis=0)
         return grad_right, grad_lower
 

time: 307 us -> 307 us (level)
  no operation moved by 1% of the time
where the time goes in v8:
time: 307 us; the launch traced here: 302 us
  Pallas kernels  299 us (97%)
    pallas_call x1, Pallas kernels, per_device(): pl.pallas_call(kernel, out_shape=(jax.ShapeDtypeStruct(grad_out.shape, bf...  290 us
    pallas_call x1, Pallas kernels, per_device(): pl.pallas_call(copy_kernel, out_shape=jax.ShapeDtypeStruct(grad_out.shape...  9.31 us
  transfers between devices with their start and end apart: 1, of which 0 were waited for; matrix products, arithmetic and copies ran while one was open for 0% of the time, Pallas kernels for 3%

profile of v8, /device:TPU:0, one launch (start us, length us, event | category | flops | bytes accessed | tf_op | source)
XLA Modules:
  0.0 302.4 jit_solution(9708988364406520088)
XLA Ops:
  0.6 289.8 %shard_map.50 = (bf16[1536,4096]{1,0:T(8,128)(2,1)}, bf16[12,256,256]{2,1,0:T(8,128)(2,1)}, bf16[6,256,256]{2,1,0:T(8,128)(2,1)}) custom-call(bf16[1536,768]{1,0:T(8,128)(2,1)} %lower.1, bf16[1536,4096]{1,0:T(8,128)(2,1)} %right.1, bf16[1536,4096]{1,0:T(8,128)(2,1)} %grad.1), custom_call_target="tpu_custom_call" | custom-call | tf_op jit(solution)/shard_map/pallas_call | solution.py:533
  290.4 0.7 collective-permute-start
  291.2 0.0 copy-start
  291.2 9.3 %shard_map.51 = bf16[1536,4096]{1,0:T(8,128)(2,1)} custom-call(bf16[1536,4096]{1,0:T(8,128)(2,1)} %get-tuple-element.10.source), custom_call_target="tpu_custom_call" | custom-call | flops 10000000000 | bytes 25165824 | tf_op jit(solution)/shard_map/pallas_call | solution.py:551
  300.5 0.0 collective-permute-done
  300.5 0.0 copy-done
  300.5 0.1 slice_select_fusion
  300.6 0.1 slice_bitcast_fusion
  300.8 0.1 maximum_dynamic-update-slice_fusion.3
  300.9 0.1 maximum_dynamic-update-slice_fusion.2
  301.0 0.0 copy-start.1
  301.0 1.4 copy-done.1
  (7 shorter events, 0.2 us)
Async XLA Ops:
  290.4 10.1 %collective-permute-start = (bf16[6,256,256]{2,1,0:T(8,128)(2,1)}, bf16[6,256,256]{2,1,0:T(8,128)(2,1)S(1)}, u32[]{:S(2)}, u32[]{:S(2)}) collective-permute-start(bf16[6,256,256]{2,1,0:T(8,128)(2,1)} %get-tuple-element.12), channel_id=1, source_target_pairs={{5,1},{7,3}} | collective-permute-start | bytes 2359304 | tf_op jit(solution)/shard_map/ppermute | solution.py:559
  291.2 9.3 %copy-start = (bf16[12,256,256]{2,1,0:T(8,128)(2,1)S(1)}, bf16[12,256,256]{2,1,0:T(8,128)(2,1)}, u32[]{:S(2)}) copy-start(bf16[12,256,256]{2,1,0:T(8,128)(2,1)} %get-tuple-element.11) | copy-start | bytes 4718596
  301.0 1.4 copy-start.1

commit v9 on v8

--- a/solution.py
+++ b/solution.py
@@ -73,15 +73,15 @@
 
     def detour(k):
         source, target, where = (
-            (fin_same.at[pl.ds(9, 3)], fin_cross.at[pl.ds(0, 3)], to_chip),
-            (fin_cross.at[pl.ds(0, 3)], fin_same.at[pl.ds(0, 3)], to_row),
-            (fin_same.at[pl.ds(0, 3)], lower_v.at[0, 1, pl.ds(9, 3)], to_chip))[k]
+            (fin_same.at[pl.ds(8, 4)], fin_cross.at[pl.ds(0, 4)], to_chip),
+            (fin_cross.at[pl.ds(0, 4)], fin_same.at[pl.ds(0, 4)], to_row),
+            (fin_same.at[pl.ds(0, 4)], lower_v.at[0, 1, pl.ds(8, 4)], to_chip))[k]
         return remote(source, target, detour_send.at[k], detour_recv.at[k], where)
 
     def cross_cases(sender_row, act):
         for case, counts in ((sender_row == 0, (5, 5, 4)),
-                             (jnp.logical_and(sender_row == 1, x == 0), (4, 4, 5)),
-                             (jnp.logical_and(sender_row == 1, x == 1), (3, 3, 6))):
+                             (jnp.logical_and(sender_row == 1, x == 0), (4, 4, 4)),
+                             (jnp.logical_and(sender_row == 1, x == 1), (4, 4, 5))):
             @pl.when(case)
             def _(counts=counts):
                 act(*counts)

time: 307 us -> 306 us (level)
  no operation moved by 1% of the time
where the time goes in v9:
time: 306 us; the launch traced here: 302 us
  Pallas kernels  299 us (98%)
    pallas_call x1, Pallas kernels, per_device(): pl.pallas_call(kernel, out_shape=(jax.ShapeDtypeStruct(grad_out.shape, bf...  290 us
    pallas_call x1, Pallas kernels, per_device(): pl.pallas_call(copy_kernel, out_shape=jax.ShapeDtypeStruct(grad_out.shape...  9.31 us
  transfers between devices with their start and end apart: 1, of which 0 were waited for; matrix products, arithmetic and copies ran while one was open for 0% of the time, Pallas kernels for 3%

profile of v9, /device:TPU:0, one launch (start us, length us, event | category | flops | bytes accessed | tf_op | source)
XLA Modules:
  0.0 302.4 jit_solution(11020370717217868950)
XLA Ops:
  0.6 289.8 %shard_map.50 = (bf16[1536,4096]{1,0:T(8,128)(2,1)}, bf16[12,256,256]{2,1,0:T(8,128)(2,1)}, bf16[6,256,256]{2,1,0:T(8,128)(2,1)}) custom-call(bf16[1536,768]{1,0:T(8,128)(2,1)} %lower.1, bf16[1536,4096]{1,0:T(8,128)(2,1)} %right.1, bf16[1536,4096]{1,0:T(8,128)(2,1)} %grad.1), custom_call_target="tpu_custom_call" | custom-call | tf_op jit(solution)/shard_map/pallas_call | solution.py:533
  290.4 0.7 collective-permute-start
  291.2 0.0 copy-start
  291.2 9.3 %shard_map.51 = bf16[1536,4096]{1,0:T(8,128)(2,1)} custom-call(bf16[1536,4096]{1,0:T(8,128)(2,1)} %get-tuple-element.10.source), custom_call_target="tpu_custom_call" | custom-call | flops 10000000000 | bytes 25165824 | tf_op jit(solution)/shard_map/pallas_call | solution.py:551
  300.5 0.0 collective-permute-done
  300.5 0.0 copy-done
  300.5 0.1 slice_select_fusion
  300.6 0.1 slice_bitcast_fusion
  300.8 0.1 maximum_dynamic-update-slice_fusion.3
  300.9 0.1 maximum_dynamic-update-slice_fusion.2
  301.0 0.0 copy-start.1
  301.0 1.4 copy-done.1
  (7 shorter events, 0.2 us)
Async XLA Ops:
  290.4 10.1 %collective-permute-start = (bf16[6,256,256]{2,1,0:T(8,128)(2,1)}, bf16[6,256,256]{2,1,0:T(8,128)(2,1)S(1)}, u32[]{:S(2)}, u32[]{:S(2)}) collective-permute-start(bf16[6,256,256]{2,1,0:T(8,128)(2,1)} %get-tuple-element.12), channel_id=1, source_target_pairs={{5,1},{7,3}} | collective-permute-start | bytes 2359304 | tf_op jit(solution)/shard_map/ppermute | solution.py:559
  291.2 9.3 %copy-start = (bf16[12,256,256]{2,1,0:T(8,128)(2,1)S(1)}, bf16[12,256,256]{2,1,0:T(8,128)(2,1)}, u32[]{:S(2)}) copy-start(bf16[12,256,256]{2,1,0:T(8,128)(2,1)} %get-tuple-element.11) | copy-start | bytes 4718596
  301.0 1.4 copy-start.1

commit v10 on v9

--- a/solution.py
+++ b/solution.py
@@ -19,7 +19,8 @@
 RETURNED = 6
 SPARE = (0, 3)
 RETURNED_FROM = 5
-COPY_PARTS = 12
+COPY_ENDS = (0, 32, 64, 128, 256, 384, 512, 640, 768, 896, 1024, 1152, 1280, 1408, 1536)
+COPY_PARTS = len(COPY_ENDS) - 1
 
 
 def dot_nt(lhs, rhs):
@@ -131,7 +132,7 @@
         fin_cross[9:] = jnp.zeros((3, BLOCK, BLOCK), jnp.bfloat16)
 
     barrier = pltpu.get_barrier_semaphore()
-    for where in (to_row, to_core, to_chip, to_diag):
+    for where in (to_diag, to_row, to_chip, to_core):
         pl.semaphore_signal(barrier, inc=1, device_id=where, device_id_type=MESH)
     pl.semaphore_wait(barrier, 4)
 
@@ -506,8 +507,7 @@
 
 
 def copy_kernel(source, target, buffer, read_sem, write_sem):
-    rows = source.shape[0] // COPY_PARTS
-    part = lambda ref, k: ref.at[pl.ds(k * rows, rows)]
+    part = lambda ref, k: ref.at[pl.ds(COPY_ENDS[k], COPY_ENDS[k + 1] - COPY_ENDS[k])]
     reads = [pltpu.make_async_copy(part(source, k), part(buffer, k), read_sem.at[k]) for k in range(COPY_PARTS)]
     writes = [pltpu.make_async_copy(part(buffer, k), part(target, k), write_sem.at[k]) for k in range(COPY_PARTS)]
     for read in reads:

time: 306 us -> 306 us (level)
  no operation moved by 1% of the time
where the time goes in v10:
time: 306 us; the launch traced here: 302 us
  Pallas kernels  299 us (98%)
    pallas_call x1, Pallas kernels, per_device(): pl.pallas_call(kernel, out_shape=(jax.ShapeDtypeStruct(grad_out.shape, bf...  290 us
    pallas_call x1, Pallas kernels, per_device(): pl.pallas_call(copy_kernel, out_shape=jax.ShapeDtypeStruct(grad_out.shape...  9.28 us
  transfers between devices with their start and end apart: 1, of which 0 were waited for; matrix products, arithmetic and copies ran while one was open for 0% of the time, Pallas kernels for 3%

profile of v10, /device:TPU:0, one launch (start us, length us, event | category | flops | bytes accessed | tf_op | source)
XLA Modules:
  0.0 302.4 jit_solution(4541202424060701093)
XLA Ops:
  0.6 289.8 %shard_map.50 = (bf16[1536,4096]{1,0:T(8,128)(2,1)}, bf16[12,256,256]{2,1,0:T(8,128)(2,1)}, bf16[6,256,256]{2,1,0:T(8,128)(2,1)}) custom-call(bf16[1536,768]{1,0:T(8,128)(2,1)} %lower.1, bf16[1536,4096]{1,0:T(8,128)(2,1)} %right.1, bf16[1536,4096]{1,0:T(8,128)(2,1)} %grad.1), custom_call_target="tpu_custom_call" | custom-call | tf_op jit(solution)/shard_map/pallas_call | solution.py:533
  290.4 0.7 collective-permute-start
  291.2 0.0 copy-start
  291.2 9.3 %shard_map.51 = bf16[1536,4096]{1,0:T(8,128)(2,1)} custom-call(bf16[1536,4096]{1,0:T(8,128)(2,1)} %get-tuple-element.10.source), custom_call_target="tpu_custom_call" | custom-call | flops 10000000000 | bytes 25165824 | tf_op jit(solution)/shard_map/pallas_call | solution.py:551
  300.5 0.0 collective-permute-done
  300.5 0.0 copy-done
  300.5 0.1 slice_select_fusion
  300.6 0.1 slice_bitcast_fusion
  300.8 0.1 maximum_dynamic-update-slice_fusion.3
  300.9 0.1 maximum_dynamic-update-slice_fusion.2
  301.0 0.0 copy-start.1
  301.0 1.4 copy-done.1
  (7 shorter events, 0.2 us)
Async XLA Ops:
  290.4 10.1 %collective-permute-start = (bf16[6,256,256]{2,1,0:T(8,128)(2,1)}, bf16[6,256,256]{2,1,0:T(8,128)(2,1)S(1)}, u32[]{:S(2)}, u32[]{:S(2)}) collective-permute-start(bf16[6,256,256]{2,1,0:T(8,128)(2,1)} %get-tuple-element.12), channel_id=1, source_target_pairs={{5,1},{7,3}} | collective-permute-start | bytes 2359304 | tf_op jit(solution)/shard_map/ppermute | solution.py:559
  291.2 9.3 %copy-start = (bf16[12,256,256]{2,1,0:T(8,128)(2,1)S(1)}, bf16[12,256,256]{2,1,0:T(8,128)(2,1)}, u32[]{:S(2)}) copy-start(bf16[12,256,256]{2,1,0:T(8,128)(2,1)} %get-tuple-element.11) | copy-start | bytes 4718596
  301.0 1.4 copy-start.1

commit v11 on v10

--- a/solution.py
+++ b/solution.py
@@ -10,9 +10,9 @@
 NUM = 6
 COLS = 4096
 TILE = 512
-LAST = 1024
-NEAR = (0, 1)
-FAR = (2, 3)
+LAST = 512
+NEAR = (0, 1, 2, 3)
+FAR = (4, 5, 6, 7)
 VMEM_BYTES = 67043328
 HOP_START = (0, 1, 2, 4, 6, 9)
 PLACE = {(1, 0): 0, (2, 0): 1, (3, 0): 2, (3, 1): 3, (4, 0): 4, (4, 1): 5, (5, 0): 6, (5, 1): 7, (5, 2): 8, (0, 0): 9, (2, 1): 10, (4, 2): 11}

time: 306 us -> 306 us (level)
  no operation moved by 1% of the time
where the time goes in v11:
time: 306 us; the launch traced here: 302 us
  Pallas kernels  299 us (98%)
    pallas_call x1, Pallas kernels, per_device(): pl.pallas_call(kernel, out_shape=(jax.ShapeDtypeStruct(grad_out.shape, bf...  290 us
    pallas_call x1, Pallas kernels, per_device(): pl.pallas_call(copy_kernel, out_shape=jax.ShapeDtypeStruct(grad_out.shape...  9.28 us
  transfers between devices with their start and end apart: 1, of which 0 were waited for; matrix products, arithmetic and copies ran while one was open for 0% of the time, Pallas kernels for 3%

profile of v11, /device:TPU:0, one launch (start us, length us, event | category | flops | bytes accessed | tf_op | source)
XLA Modules:
  0.0 302.3 jit_solution(13098187385706117987)
XLA Ops:
  0.6 289.7 %shard_map.50 = (bf16[1536,4096]{1,0:T(8,128)(2,1)}, bf16[12,256,256]{2,1,0:T(8,128)(2,1)}, bf16[6,256,256]{2,1,0:T(8,128)(2,1)}) custom-call(bf16[1536,768]{1,0:T(8,128)(2,1)} %lower.1, bf16[1536,4096]{1,0:T(8,128)(2,1)} %right.1, bf16[1536,4096]{1,0:T(8,128)(2,1)} %grad.1), custom_call_target="tpu_custom_call" | custom-call | tf_op jit(solution)/shard_map/pallas_call | solution.py:533
  290.3 0.7 collective-permute-start
  291.1 0.0 copy-start
  291.1 9.3 %shard_map.51 = bf16[1536,4096]{1,0:T(8,128)(2,1)} custom-call(bf16[1536,4096]{1,0:T(8,128)(2,1)} %get-tuple-element.10.source), custom_call_target="tpu_custom_call" | custom-call | flops 10000000000 | bytes 25165824 | tf_op jit(solution)/shard_map/pallas_call | solution.py:551
  300.4 0.0 collective-permute-done
  300.4 0.0 copy-done
  300.4 0.1 slice_select_fusion
  300.5 0.1 slice_bitcast_fusion
  300.7 0.1 maximum_dynamic-update-slice_fusion.3
  300.8 0.1 maximum_dynamic-update-slice_fusion.2
  300.9 0.0 copy-start.1
  300.9 1.4 copy-done.1
  (7 shorter events, 0.2 us)
Async XLA Ops:
  290.3 10.1 %collective-permute-start = (bf16[6,256,256]{2,1,0:T(8,128)(2,1)}, bf16[6,256,256]{2,1,0:T(8,128)(2,1)S(1)}, u32[]{:S(2)}, u32[]{:S(2)}) collective-permute-start(bf16[6,256,256]{2,1,0:T(8,128)(2,1)} %get-tuple-element.12), channel_id=1, source_target_pairs={{5,1},{7,3}} | collective-permute-start | bytes 2359304 | tf_op jit(solution)/shard_map/ppermute | solution.py:559
  291.1 9.3 %copy-start = (bf16[12,256,256]{2,1,0:T(8,128)(2,1)S(1)}, bf16[12,256,256]{2,1,0:T(8,128)(2,1)}, u32[]{:S(2)}) copy-start(bf16[12,256,256]{2,1,0:T(8,128)(2,1)} %get-tuple-element.11) | copy-start | bytes 4718596
  300.9 1.4 copy-start.1
